TPU v7x, 32 devices: a whole 2x2x4 slice. The times are simulated.
32 devices in a mesh: dp: 8 (over z, y), tensor: 4 (over x, core).
Axes of the slice: x: 2, y: 2, z: 4, core: 2. Of those that a mesh axis runs over, the one named last changes fastest.
Arguments:
- tokens: bfloat16 [8192, 1024], P('dp'), may hold values from -6 to 6
- w_query: bfloat16 [1024, 1024], P(None, 'tensor'), may hold values from -0.25 to 0.25
- key_weight: bfloat16 [1024, 512], P(None, 'tensor'), may hold values from -0.25 to 0.25
- value_weight: bfloat16 [1024, 512], P(None, 'tensor'), may hold values from -0.1875 to 0.1875
- w_output: bfloat16 [1024, 1024], P('tensor'), may hold values from -1 to 1
- gain_attn: float32 [1024], replicated, may hold values from 0.5 to 1.5
- gain_ffn: float32 [1024], replicated, may hold values from 0.5 to 1.5
- router: bfloat16 [1024, 16], replicated, may hold values from -0.09375 to 0.09375
- w_gate: bfloat16 [16, 1024, 512], P(None, None, 'tensor'), may hold values from -0.1875 to 0.1875
- w_up: bfloat16 [16, 1024, 512], P(None, None, 'tensor'), may hold values from -0.1875 to 0.1875
- w_down: bfloat16 [16, 512, 1024], P(None, 'tensor'), may hold values from -1 to 1
- piece_start: int32 [8, 2], P('dp'), may hold values from 0 to 768, as said below
- piece_kind: int32 [8, 2], P('dp'), may hold values from 0 to 1
- choices: int32 [8192, 8], P('dp'), may hold values from 0 to 15, all different within a row
- place_order: int32 [8, 1024], P('dp'), may hold values from 0 to 1023, each once within a row
- cotangent: bfloat16 [8192, 1024], P('dp'), may hold values from -6 to 6
Outputs:
- output: bfloat16 [8192, 1024], P('dp')
- input_grad: bfloat16 [8192, 1024], P('dp')
- grad_query: float32 [1024, 1024], P('dp', 'tensor')
- grad_key: float32 [1024, 512], P('dp', 'tensor')
- grad_value: float32 [1024, 512], P('dp', 'tensor')
- grad_output: float32 [1024, 1024], P('tensor', 'dp')
- grad_gain_attn: float32 [1024], P('dp')
- grad_gain_ffn: float32 [1024], P('dp')
- grad_router: float32 [1024, 16], P('dp')
- grad_gate: float32 [16, 1024, 512], P(None, 'dp', 'tensor')
- grad_up: float32 [16, 1024, 512], P(None, 'dp', 'tensor')
- grad_down: float32 [16, 512, 1024], P(None, 'tensor', 'dp')
Inputs may be any that keep to these rules, and one draw needn't show every extreme that they name: `piece_start`: slot k of a sequence starts in [k * 512, (k + 1) * 512 - 256], so pieces never meet. `choices`: each row names 8 different experts. `place_order`: each row is a permutation of 0 to 1023.
All inputs are finite; a program needn't handle non-finite values.
Results may differ from a plain program's by a relative error of at most 0.025.
Values may be sent and summed in bfloat16 or wider, within the bound.
A program may use at most 384 MiB of HBM per device.

v0:
```python
import jax
import jax.numpy as jnp
from jax import lax
from jax.sharding import PartitionSpec as P

MODEL_WIDTH = 1024
HEAD_SIZE = 64
TOP = 8
E = 16
PIECE = 256
QBLK = 512
CAP = 640


epsilon = 1e-06
negative = -1e30


def rope_tables(sequence_length):
    half_width = HEAD_SIZE // 2
    frequency = 10000.0 ** (-(jnp.arange(half_width, dtype=jnp.float32) * 2.0 / HEAD_SIZE))
    angles = jnp.arange(sequence_length, dtype=jnp.float32)[:, None] * frequency[None, :]
    return (jnp.cos(angles), jnp.sin(angles))


def apply_rotation(values, cosine_table, sine_values):
    half_width = HEAD_SIZE // 2
    first = values[..., :half_width]
    second = values[..., half_width:]
    cos_part = cosine_table[:, None, :]
    sin_part = sine_values[:, None, :]
    return jnp.concatenate(
        [first * cos_part - second * sin_part, second * cos_part + first * sin_part], axis=-1
    )


def unrotate(grads, cosine_table, sine_values):
    half_width = HEAD_SIZE // 2
    first = grads[..., :half_width]
    second = grads[..., half_width:]
    cos_part = cosine_table[:, None, :]
    sin_part = sine_values[:, None, :]
    return jnp.concatenate(
        [first * cos_part + second * sin_part, second * cos_part - first * sin_part], axis=-1
    )


def allowed(starts, kind_row, row_pos, col_pos):
    ends = starts + PIECE
    inside_row = (
        (kind_row[None, :] == 1)
        & (row_pos[:, None] >= starts[None, :])
        & (row_pos[:, None] < ends[None, :])
    )
    inside_col = (
        (kind_row[None, :] == 1)
        & (col_pos[:, None] >= starts[None, :])
        & (col_pos[:, None] < ends[None, :])
    )
    same_piece = jnp.any(inside_row[:, None, :] & inside_col[None, :, :], axis=-1)
    return (col_pos[None, :] <= row_pos[:, None]) | same_piece


def slot_table(pick_rows, rank_rows):
    sequence_length = pick_rows.shape[0]
    inverse = (
        jnp.zeros((sequence_length,), jnp.int32)
        .at[rank_rows]
        .set(jnp.arange(sequence_length, dtype=jnp.int32))
    )
    ranked = pick_rows[inverse].reshape(-1)
    onehot = (ranked[:, None] == jnp.arange(E, dtype=jnp.int32)[None, :]).astype(jnp.int32)
    before = jnp.cumsum(onehot, axis=0) - onehot
    return jnp.sum(before * onehot, axis=1).reshape(sequence_length, TOP)[rank_rows]


def routing(pick_rows, rank_rows):
    sequence_length = pick_rows.shape[0]
    slot_index = slot_table(pick_rows, rank_rows)
    kept = slot_index < CAP
    flat_index = jnp.where(kept, pick_rows * CAP + slot_index, E * CAP)
    owners = jnp.broadcast_to(
        jnp.arange(sequence_length, dtype=jnp.int32)[:, None], pick_rows.shape
    )
    token_table = (
        jnp.full((E * CAP + 1,), sequence_length, jnp.int32)
        .at[flat_index.reshape(-1)]
        .set(owners.reshape(-1))
    )
    return (flat_index, kept, token_table[: E * CAP])


def body(
    tokens,
    w_query,
    key_weight,
    value_weight,
    w_output,
    gain_attn,
    gain_ffn,
    router,
    w_gate,
    w_up,
    w_down,
    piece_start,
    piece_kind,
    choices,
    place_order,
    cotangent,
):
    row_count = tokens.shape[0]
    seq_count = piece_start.shape[0]
    sequence_length = row_count // seq_count
    kv_local = key_weight.shape[1] // HEAD_SIZE
    q_local = w_query.shape[1] // HEAD_SIZE
    ff_local = w_gate.shape[2]
    group_size = q_local // kv_local
    per_seq = sequence_length // QBLK
    scale = HEAD_SIZE ** (-0.5)
    slot_count = seq_count * E * CAP
    seq_range = jnp.arange(seq_count, dtype=jnp.int32)
    resid_in = tokens.astype(jnp.float32)
    grad_out = cotangent.astype(jnp.float32)
    inv_one = lax.rsqrt(jnp.mean(resid_in * resid_in, axis=1, keepdims=True) + epsilon)
    first_normed = (resid_in * inv_one * gain_attn).astype(jnp.bfloat16)
    cosine_table, sine_values = rope_tables(sequence_length)
    cos_rows = jnp.tile(cosine_table, (seq_count, 1))
    sin_rows = jnp.tile(sine_values, (seq_count, 1))
    query_unrotated = jnp.dot(first_normed, w_query, preferred_element_type=jnp.float32).reshape(
        row_count, q_local, HEAD_SIZE
    )
    query_rows = (
        apply_rotation(query_unrotated, cos_rows, sin_rows)
        .astype(jnp.bfloat16)
        .reshape(seq_count, sequence_length, kv_local, group_size, HEAD_SIZE)
    )
    key_unrotated = jnp.dot(first_normed, key_weight, preferred_element_type=jnp.float32).reshape(
        row_count, kv_local, HEAD_SIZE
    )
    key_rows = (
        apply_rotation(key_unrotated, cos_rows, sin_rows)
        .astype(jnp.bfloat16)
        .reshape(seq_count, sequence_length, kv_local, HEAD_SIZE)
    )
    value_matrix_rows = (
        jnp.dot(first_normed, value_weight, preferred_element_type=jnp.float32)
        .astype(jnp.bfloat16)
        .reshape(seq_count, sequence_length, kv_local, HEAD_SIZE)
    )

    def block_scores(seq_index, block_index):
        start_row = block_index * QBLK
        key_length = start_row + QBLK
        query_block = query_rows[seq_index, start_row : start_row + QBLK]
        key_block = key_rows[seq_index, :key_length]
        value_block = value_matrix_rows[seq_index, :key_length]
        scores = (
            jnp.einsum("qgrd,kgd->grqk", query_block, key_block, preferred_element_type=jnp.float32)
            * scale
        )
        visible = allowed(
            piece_start[seq_index],
            piece_kind[seq_index],
            start_row + jnp.arange(QBLK, dtype=jnp.int32),
            jnp.arange(key_length, dtype=jnp.int32),
        )
        scores = jnp.where(visible[None, None], scores, negative)
        return (scores, query_block, key_block, value_block)

    head_pieces = []
    total_pieces = []
    for block_index in range(per_seq):

        def forward_block(seq_index, block_index=block_index):
            scores, query_block, key_block, value_block = block_scores(seq_index, block_index)
            top_score = jnp.max(scores, axis=-1, keepdims=True)
            log_total = top_score + jnp.log(
                jnp.sum(jnp.exp(scores - top_score), axis=-1, keepdims=True)
            )
            attn_probs = jnp.exp(scores - log_total).astype(jnp.bfloat16)
            result = jnp.einsum(
                "grqk,kgd->qgrd", attn_probs, value_block, preferred_element_type=jnp.float32
            )
            return (result.astype(jnp.bfloat16), log_total[..., 0])

        result_block, total_block = lax.map(forward_block, seq_range)
        head_pieces.append(result_block)
        total_pieces.append(total_block)
    head_out = jnp.concatenate(head_pieces, axis=1).reshape(row_count, q_local * HEAD_SIZE)
    attn_part = jnp.dot(head_out, w_output, preferred_element_type=jnp.float32)
    resid_mid = resid_in + lax.psum(attn_part.astype(jnp.bfloat16), "tensor").astype(jnp.float32)
    inv_two = lax.rsqrt(jnp.mean(resid_mid * resid_mid, axis=1, keepdims=True) + epsilon)
    normed_two = (resid_mid * inv_two * gain_ffn).astype(jnp.bfloat16)
    logits = jnp.dot(normed_two, router, preferred_element_type=jnp.float32)
    pick_hot = (choices[:, :, None] == jnp.arange(E, dtype=jnp.int32)[None, None, :]).astype(
        jnp.float32
    )
    chosen = jnp.sum(pick_hot * logits[:, None, :], axis=-1)
    gate_probs = jax.nn.softmax(chosen, axis=1)
    flat_local, kept_local, table_local = jax.vmap(routing)(
        choices.reshape(seq_count, sequence_length, TOP), place_order
    )
    global_flat = jnp.where(
        kept_local, flat_local + seq_range[:, None, None] * (E * CAP), slot_count
    ).reshape(row_count, TOP)
    kept_mask = kept_local.reshape(row_count, TOP).astype(jnp.float32)
    token_table = jnp.where(
        table_local < sequence_length, table_local + seq_range[:, None] * sequence_length, row_count
    ).reshape(-1)
    weight_pair = jnp.concatenate([w_gate, w_up], axis=2)
    dispatched = jnp.take(normed_two, token_table, axis=0, mode="fill", fill_value=0).reshape(
        seq_count, E, CAP, MODEL_WIDTH
    )
    both_pre = jnp.einsum(
        "secd,edf->secf", dispatched, weight_pair, preferred_element_type=jnp.float32
    )
    gate_pre = both_pre[..., :ff_local]
    up_pre = both_pre[..., ff_local:]
    sigmoid = jax.nn.sigmoid(gate_pre)
    activated = gate_pre * sigmoid
    hidden = (activated * up_pre).astype(jnp.bfloat16)
    expert_part = jnp.einsum(
        "secf,efd->secd", hidden, w_down, preferred_element_type=jnp.float32
    ).reshape(slot_count, MODEL_WIDTH)
    slot_gate = gate_probs * kept_mask
    gate_table = (
        jnp.zeros((slot_count + 1,), jnp.float32)
        .at[global_flat.reshape(-1)]
        .set(slot_gate.reshape(-1))[:slot_count]
    )
    combined = jax.ops.segment_sum(
        gate_table[:, None] * expert_part, token_table, num_segments=row_count + 1
    )[:row_count]
    slot_grad = jnp.take(cotangent, token_table, axis=0, mode="fill", fill_value=0)
    slot_dot = jnp.sum(slot_grad.astype(jnp.float32) * expert_part, axis=1)
    grad_gate_part = jnp.take(slot_dot, global_flat, axis=0, mode="fill", fill_value=0) * kept_mask
    moe_full = lax.psum(combined.astype(jnp.bfloat16), "tensor").astype(jnp.float32)
    output = (resid_mid + moe_full).astype(jnp.bfloat16)
    grad_expert = (
        (gate_table[:, None] * slot_grad.astype(jnp.float32))
        .astype(jnp.bfloat16)
        .reshape(seq_count, E, CAP, MODEL_WIDTH)
    )
    grad_hidden = jnp.einsum(
        "secd,efd->secf", grad_expert, w_down, preferred_element_type=jnp.float32
    )
    grad_down = jnp.einsum(
        "secf,secd->efd", hidden, grad_expert, preferred_element_type=jnp.float32
    )
    silu_slope = sigmoid * (1.0 + gate_pre * (1.0 - sigmoid))
    grad_gate_pre = (grad_hidden * up_pre * silu_slope).astype(jnp.bfloat16)
    grad_up_pre = (grad_hidden * activated).astype(jnp.bfloat16)
    grad_gate = jnp.einsum(
        "secd,secf->edf", dispatched, grad_gate_pre, preferred_element_type=jnp.float32
    )
    grad_up = jnp.einsum(
        "secd,secf->edf", dispatched, grad_up_pre, preferred_element_type=jnp.float32
    )
    grad_pair = jnp.concatenate([grad_gate_pre, grad_up_pre], axis=3)
    grad_disp = jnp.einsum(
        "secf,edf->secd", grad_pair, weight_pair, preferred_element_type=jnp.float32
    ).reshape(slot_count, MODEL_WIDTH)
    normed_part = jax.ops.segment_sum(grad_disp, token_table, num_segments=row_count + 1)[
        :row_count
    ]
    normed_sum, grad_gate_full = (
        lax.psum(normed_part.astype(jnp.bfloat16), "tensor").astype(jnp.float32),
        lax.psum(grad_gate_part.astype(jnp.bfloat16), "tensor").astype(jnp.float32),
    )
    grad_chosen = gate_probs * (
        grad_gate_full - jnp.sum(gate_probs * grad_gate_full, axis=1, keepdims=True)
    )
    grad_logits = jnp.sum(pick_hot * grad_chosen[:, :, None], axis=1).astype(jnp.bfloat16)
    grad_normed_two = normed_sum + jnp.einsum(
        "te,de->td", grad_logits, router, preferred_element_type=jnp.float32
    )
    grad_router = jnp.einsum(
        "td,te->de", normed_two, grad_logits, preferred_element_type=jnp.float32
    )
    grad_gain_ffn = jnp.sum(grad_normed_two * resid_mid * inv_two, axis=0)
    scaled_two = gain_ffn * grad_normed_two
    grad_mid = (
        grad_out
        + inv_two * scaled_two
        - resid_mid * inv_two**3 * jnp.mean(scaled_two * resid_mid, axis=1, keepdims=True)
    )
    grad_attn = grad_mid.astype(jnp.bfloat16)
    grad_output = jnp.einsum("tf,td->fd", head_out, grad_attn, preferred_element_type=jnp.float32)
    grad_heads = jnp.einsum(
        "td,fd->tf", grad_attn, w_output, preferred_element_type=jnp.float32
    ).astype(jnp.bfloat16)
    grad_heads = grad_heads.reshape(seq_count, sequence_length, kv_local, group_size, HEAD_SIZE)
    query_pieces = []
    grad_keys = jnp.zeros((seq_count, sequence_length, kv_local, HEAD_SIZE), jnp.float32)
    grad_values = jnp.zeros((seq_count, sequence_length, kv_local, HEAD_SIZE), jnp.float32)
    for block_index in range(per_seq):

        def backward_block(seq_index, block_index=block_index):
            scores, query_block, key_block, value_block = block_scores(seq_index, block_index)
            start_row = block_index * QBLK
            probs_full = jnp.exp(scores - total_pieces[block_index][seq_index][..., None])
            probs_low = probs_full.astype(jnp.bfloat16)
            grad_block = grad_heads[seq_index, start_row : start_row + QBLK]
            grad_probs = jnp.einsum(
                "qgrd,kgd->grqk", grad_block, value_block, preferred_element_type=jnp.float32
            )
            delta = jnp.sum(probs_full * grad_probs, axis=-1, keepdims=True)
            grad_scores = (probs_full * (grad_probs - delta)).astype(jnp.bfloat16)
            grad_queries = (
                jnp.einsum(
                    "grqk,kgd->qgrd", grad_scores, key_block, preferred_element_type=jnp.float32
                )
                * scale
            )
            key_part = (
                jnp.einsum(
                    "grqk,qgrd->kgd", grad_scores, query_block, preferred_element_type=jnp.float32
                )
                * scale
            )
            value_part = jnp.einsum(
                "grqk,qgrd->kgd", probs_low, grad_block, preferred_element_type=jnp.float32
            )
            return (grad_queries, key_part, value_part)

        query_block_grad, key_block_grad, value_block_grad = lax.map(backward_block, seq_range)
        query_pieces.append(query_block_grad)
        missing = sequence_length - (block_index + 1) * QBLK
        grad_keys = grad_keys + jnp.pad(key_block_grad, ((0, 0), (0, missing), (0, 0), (0, 0)))
        grad_values = grad_values + jnp.pad(
            value_block_grad, ((0, 0), (0, missing), (0, 0), (0, 0))
        )
    grad_queries = jnp.concatenate(query_pieces, axis=1)
    grad_q_pre = (
        unrotate(grad_queries.reshape(row_count, q_local, HEAD_SIZE), cos_rows, sin_rows)
        .astype(jnp.bfloat16)
        .reshape(row_count, q_local * HEAD_SIZE)
    )
    grad_k_pre = (
        unrotate(grad_keys.reshape(row_count, kv_local, HEAD_SIZE), cos_rows, sin_rows)
        .astype(jnp.bfloat16)
        .reshape(row_count, kv_local * HEAD_SIZE)
    )
    grad_v_pre = grad_values.astype(jnp.bfloat16).reshape(row_count, kv_local * HEAD_SIZE)
    grad_query = jnp.einsum(
        "td,tf->df", first_normed, grad_q_pre, preferred_element_type=jnp.float32
    )
    grad_key = jnp.einsum("td,tf->df", first_normed, grad_k_pre, preferred_element_type=jnp.float32)
    grad_value = jnp.einsum(
        "td,tf->df", first_normed, grad_v_pre, preferred_element_type=jnp.float32
    )
    normed_one_part = jnp.einsum(
        "tf,df->td", grad_q_pre, w_query, preferred_element_type=jnp.float32
    )
    normed_one_part = normed_one_part + jnp.einsum(
        "tf,df->td", grad_k_pre, key_weight, preferred_element_type=jnp.float32
    )
    normed_one_part = normed_one_part + jnp.einsum(
        "tf,df->td", grad_v_pre, value_weight, preferred_element_type=jnp.float32
    )
    grad_normed_one = lax.psum(normed_one_part.astype(jnp.bfloat16), "tensor").astype(jnp.float32)
    grad_gain_attn = jnp.sum(grad_normed_one * resid_in * inv_one, axis=0)
    scaled_one = gain_attn * grad_normed_one
    input_grad = (
        grad_mid
        + inv_one * scaled_one
        - resid_in * inv_one**3 * jnp.mean(scaled_one * resid_in, axis=1, keepdims=True)
    ).astype(jnp.bfloat16)
    (
        sent_query,
        sent_key,
        sent_value,
        sent_output,
        sent_gain_attn,
        sent_gain_ffn,
        sent_router,
        sent_gate,
        sent_up,
        sent_down,
    ) = (
        lax.psum_scatter(grad_query, "dp", scatter_dimension=0, tiled=True),
        lax.psum_scatter(grad_key, "dp", scatter_dimension=0, tiled=True),
        lax.psum_scatter(grad_value, "dp", scatter_dimension=0, tiled=True),
        lax.psum_scatter(grad_output, "dp", scatter_dimension=1, tiled=True),
        lax.psum_scatter(grad_gain_attn, "dp", scatter_dimension=0, tiled=True),
        lax.psum_scatter(grad_gain_ffn, "dp", scatter_dimension=0, tiled=True),
        lax.psum_scatter(grad_router, "dp", scatter_dimension=0, tiled=True),
        lax.psum_scatter(grad_gate, "dp", scatter_dimension=1, tiled=True),
        lax.psum_scatter(grad_up, "dp", scatter_dimension=1, tiled=True),
        lax.psum_scatter(grad_down, "dp", scatter_dimension=2, tiled=True),
    )
    return (
        output,
        input_grad,
        sent_query,
        sent_key,
        sent_value,
        sent_output,
        sent_gain_attn,
        sent_gain_ffn,
        sent_router,
        sent_gate,
        sent_up,
        sent_down,
    )


def solution(mesh):
    return jax.shard_map(
        body,
        mesh=mesh,
        in_specs=(
            P("dp", None),
            P(None, "tensor"),
            P(None, "tensor"),
            P(None, "tensor"),
            P("tensor", None),
            P(),
            P(),
            P(),
            P(None, None, "tensor"),
            P(None, None, "tensor"),
            P(None, "tensor", None),
            P("dp", None),
            P("dp", None),
            P("dp", None),
            P("dp", None),
            P("dp", None),
        ),
        out_specs=(
            P("dp", None),
            P("dp", None),
            P("dp", "tensor"),
            P("dp", "tensor"),
            P("dp", "tensor"),
            P("tensor", "dp"),
            P("dp"),
            P("dp"),
            P("dp", None),
            P(None, "dp", "tensor"),
            P(None, "dp", "tensor"),
            P(None, "tensor", "dp"),
        ),
        check_vma=False,
    )
```

profile of v0, /device:TPU:0, one launch (start us, length us, event | category | flops | bytes accessed | tf_op | source)
XLA Modules:
  0.0 1523.3 jit_solution(12151855459982700558)
XLA Ops:
  7.3 2.2 fusion.19
  10.6 2.2 fusion.21
  18.7 1.8 fusion.36
  21.6 1.5 convolution_convert_fusion.4
  25.4 2.7 fusion.15
  28.2 1.8 exponential_reduce_fusion
  30.1 3.3 copy-done.13
  34.6 2.2 convolution_convert_fusion.2
  37.6 2.1 convolution_convert_fusion
  39.9 4.3 scatter_custom_fusion.3
  44.5 5.1 gather_fusion.1
  50.0 4.8 reduce-window.6
  56.5 4.9 gather_fusion.2
  63.9 30.5 %scatter_custom_fusion.4 = s32[10241]{0:T(1024)S(1)} fusion(s32[8192]{0:T(1024)S(1)} %broadcast_select_fusion.3, s32[8192]{0:T(1024)S(1)} %reshape.881, s32[]{:T(128)} %constant.140.clone.1), kind=kCustom, calls=%fused_computation.183 | custom fusion | bytes 40968
  94.6 6.4 copy.130
  101.0 6.6 copy.131
  107.5 44.2 %gather_fusion.4 = bf16[10240,1024]{1,0:T(8,128)(2,1)} fusion(bf16[1024,1024]{1,0:T(8,128)(2,1)S(1)} %copy-done.3, s32[10240]{0:T(1024)S(1)} %fusion.73), kind=kCustom, calls=%fused_computation.1.clone | custom fusion | bytes 41984000 | tf_op jit(solution)/shard_map/jit(_take)/gather | solution.py:234
  151.8 3.1 multiply_reduce_fusion.2
  156.3 44.1 %gather_fusion.3 = bf16[10240,1024]{1,0:T(8,128)(2,1)} fusion(bf16[1024,1024]{1,0:T(8,128)(2,1)S(1)} %multiply_convert_fusion.1, s32[10240]{0:T(1024)S(1)} %fusion.73), kind=kCustom, calls=%fused_computation.clone | custom fusion | bytes 41984000 | tf_op jit(solution)/shard_map/jit(_take)/gather | solution.py:211
  202.3 30.5 %scatter_custom_fusion = f32[10241]{0:T(1024)S(1)} fusion(s32[8192]{0:T(1024)S(1)} %bitcast.336, f32[8192]{0:T(1024)S(1)} %reshape.900, f32[]{:T(128)} %constant.114.clone.1), kind=kCustom, calls=%fused_computation.185 | custom fusion | bytes 40968 | tf_op jit(solution)/shard_map/scatter | solution.py:229
  232.8 19.0 %broadcast_select_fusion.1 = bf16[10240,1024]{1,0:T(8,128)(2,1)} fusion(bf16[10240,1024]{1,0:T(8,128)(2,1)} %gather_fusion.3, pred[10240]{0:T(1024)(128)(4,1)S(1)} %compare_and_fusion), kind=kLoop, calls=%fused_computation.16 | loop fusion | flops 10485760 | bytes 41953280 | tf_op jit(solution)/shard_map/jit(_take)/select_n | solution.py:211
  251.8 15.3 %fusion.29 = f32[1,16,640,256]{2,3,1,0:T(8,128)} fusion(bf16[16,640,1024]{2,1,0:T(8,128)(2,1)} %bitcast.289, bf16[16,1024,128]{1,2,0:T(8,128)(2,1)S(1)} %copy-done.19, bf16[16,1024,128]{1,2,0:T(8,128)(2,1)S(1)} %copy-done.18), kind=kOutput, calls=%fused_computation.78 | convolution fusion | flops 5385486336 | bytes 39845888 | tf_op jit(solution)/shard_map/secd,edf->secf/dot_general | solution.py:214
  267.1 4.8 fusion.31
  271.9 1.6 copy-done.15
  273.5 17.9 %fusion.117 = f32[16,640,1024]{2,1,0:T(8,128)} fusion(bf16[16,640,128]{1,2,0:T(8,128)(2,1)S(1)} %fusion.31, bf16[16,128,1024]{2,1,0:T(8,128)(2,1)} %param.28), kind=kOutput, calls=%fused_computation.244 | convolution fusion | flops 2684354560 | bytes 48758784 | tf_op jit(solution)/shard_map/secf,efd->secd/dot_general | solution.py:222
  291.3 40.5 %fusion.1 = (bf16[10240]{0:T(1024)(128)(2,1)S(1)}, f32[10240,1024]{1,0:T(8,128)}, bf16[10240,1024]{1,0:T(8,128)(2,1)}) fusion(f32[16,640,1024]{2,1,0:T(8,128)} %fusion.117, bf16[10240,1024]{1,0:T(8,128)(2,1)} %gather_fusion.4, pred[10240]{0:T(1024)(128)(4,1)S(1)} %compare_and_fusion, f32[10240]{0:T(1024)S(1)} %slice-done.2), kind=kLoop, calls=%fused_computation.13 | loop fusion | flops 73390080 | bytes 125900800 | tf_op jit(solution)/shard_map/reduce_sum | solution.py:235
  331.8 16.6 %fusion.11 = (bf16[1,16,640,128]{2,3,1,0:T(8,128)(2,1)}, bf16[1,16,640,128]{2,3,1,0:T(8,128)(2,1)S(1)}) fusion(f32[1,16,640,256]{2,3,1,0:T(8,128)} %fusion.29, bf16[16,640,1024]{2,1,0:T(8,128)(2,1)} %bitcast.292, bf16[16,128,1024]{2,1,0:T(8,128)(2,1)} %param.28), kind=kOutput, calls=%fused_computation.42 | convolution fusion | flops 2701393920 | bytes 40894464 | tf_op jit(solution)/shard_map/secd,efd->secf/dot_general | solution.py:244
  348.5 19.6 %fusion.6 = f32[16,1024,640]{1,2,0:T(8,128)} fusion(bf16[16,1024,128]{1,2,0:T(8,128)(2,1)} %copy.131, bf16[16,1024,128]{1,2,0:T(8,128)(2,1)} %copy.130, bf16[1,16,640,128]{2,3,1,0:T(8,128)(2,1)S(1)} %get-tuple-element.132, bf16[1,16,640,128]{2,3,1,0:T(8,128)(2,1)} %get-tuple-element.131), kind=kOutput, calls=%fused_computation.33 | convolution fusion | flops 5395972096 | bytes 55574528 | tf_op jit(solution)/shard_map/secf,edf->secd/dot_general | solution.py:260
  368.1 90.9 %scatter_custom_fusion.2 = f32[1025,1024]{1,0:T(8,128)} fusion(s32[10240]{0:T(1024)} %bitcast.333, f32[10240,1024]{1,0:T(8,128)} %bitcast.299, f32[]{:T(128)} %constant.114.clone.1), kind=kCustom, calls=%fused_computation.86 | custom fusion | flops 10485760 | bytes 4198912 | tf_op jit(solution)/shard_map/scatter-add | solution.py:263
  459.0 3.8 slice.163
  463.4 50.7 %gather_fusion = bf16[8192]{0:T(1024)(128)(2,1)S(1)} fusion(bf16[10240]{0:T(1024)(128)(2,1)S(1)} %get-tuple-element.117, s32[8192]{0:T(1024)S(1)} %broadcast_clamp_fusion), kind=kCustom, calls=%fused_computation.2 | custom fusion | bytes 65536 | tf_op jit(solution)/shard_map/jit(_take)/gather | solution.py:236
  514.6 90.5 %scatter_custom_fusion.1 = f32[1025,1024]{1,0:T(8,128)} fusion(s32[10240]{0:T(1024)} %bitcast.334, f32[10240,1024]{1,0:T(8,128)} %get-tuple-element.118, f32[]{:T(128)} %constant.114.clone.1), kind=kCustom, calls=%fused_computation.88 | custom fusion | flops 10485760 | bytes 4198912 | tf_op jit(solution)/shard_map/scatter-add | solution.py:231
  605.1 3.8 slice.164
  608.9 12.9 psum.38
  622.1 4.1 multiply_reduce_fusion
  626.8 1.7 multiply_subtract_fusion
  629.3 2.9 copy-done.14
  633.5 1.5 fusion.26
  635.9 2.9 fusion.2
  641.4 2.4 fusion.47
  643.8 2.8 fusion.4
  650.8 2.1 add_convert_fusion
  652.9 1.5 copy-done.2
  655.5 3.3 fusion.122
  658.9 1.6 fusion.121
  660.6 4.0 fusion.50
  664.7 1.7 fusion.120
  666.5 14.7 fusion.123
  681.2 1.7 copy-done.22
  683.0 12.5 fusion.34
  695.6 1.7 copy-done.21
  697.3 13.0 fusion.32
  712.1 26.8 %all-reduce.14.cloned.1.call-done = (bf16[1024,1024]{1,0:T(8,128)(2,1)}, bf16[1024,1024]{1,0:T(8,128)(2,1)}) async-done(((bf16[1024,1024]{1,0:T(8,128)(2,1)}, bf16[1024,1024]{1,0:T(8,128)(2,1)}), (bf16[1024,1024]{1,0:T(8,128)(2,1)}, bf16[1024,1024]{1,0:T(8,128)(2,1)})) %all-reduce.14.cloned.1.call-update) | async-done | bytes 4194320 | tf_op jit(solution)/shard_map/psum | solution.py:237
  738.9 3.2 fusion.25
  742.1 21.6 %all-reduce.4 = (f32[1024]{0:T(1024)S(1)}, f32[1024]{0:T(1024)S(1)}) all-reduce(f32[1024]{0:T(1024)S(1)} %get-tuple-element.96, f32[1024]{0:T(1024)S(1)} %get-tuple-element.94), channel_id=6, replica_groups=mesh['dp'=8,'tensor'=4] {'dp'}, use_global_device_ids=true, to_apply=%region_36.38.clone | all-reduce | flops 2048 | bytes 16384
  764.9 6.3 fusion.18
  771.3 26.2 %reduce-scatter.17.cloned.1.call-done = f32[128,16]{0,1:T(8,128)} async-done(((f32[1024,16]{0,1:T(8,128)}), f32[128,16]{0,1:T(8,128)}) %reduce-scatter.17.cloned.1.call-update) | async-done | bytes 8208 | tf_op jit(solution)/shard_map/reduce_scatter | solution.py:387
  797.4 65.4 %reduce-scatter.13.cloned.1.call-done = f32[128,128]{1,0:T(8,128)} async-done(((f32[1024,128]{1,0:T(8,128)}), f32[128,128]{1,0:T(8,128)}) %reduce-scatter.13.cloned.1.call-update) | async-done | bytes 65552 | tf_op jit(solution)/shard_map/reduce_scatter | solution.py:383
  862.8 65.4 %reduce-scatter.11.cloned.1.call-done = f32[128,128]{1,0:T(8,128)} async-done(((f32[1024,128]{1,0:T(8,128)}), f32[128,128]{1,0:T(8,128)}) %reduce-scatter.11.cloned.1.call-update) | async-done | bytes 65552 | tf_op jit(solution)/shard_map/reduce_scatter | solution.py:382
  928.2 67.6 %reduce-scatter.15.cloned.1.call-done = f32[256,128]{1,0:T(8,128)} async-done(((f32[256,1024]{1,0:T(8,128)}), f32[256,128]{1,0:T(8,128)}) %reduce-scatter.15.cloned.1.call-update) | async-done | bytes 131088 | tf_op jit(solution)/shard_map/reduce_scatter | solution.py:384
  995.9 67.1 %reduce-scatter.9.cloned.1.call-done = f32[128,256]{1,0:T(8,128)} async-done(((f32[1024,256]{1,0:T(8,128)}), f32[128,256]{1,0:T(8,128)}) %reduce-scatter.9.cloned.1.call-update) | async-done | bytes 131088 | tf_op jit(solution)/shard_map/reduce_scatter | solution.py:381
  1063.0 151.1 %reduce-scatter.23.cloned.1.call-done = f32[16,128,128]{2,1,0:T(8,128)} async-done(((f32[16,128,1024]{2,1,0:T(8,128)}), f32[16,128,128]{2,1,0:T(8,128)}) %reduce-scatter.23.cloned.1.call-update) | async-done | bytes 1048592 | tf_op jit(solution)/shard_map/reduce_scatter | solution.py:390
  1214.0 151.1 %reduce-scatter.19.cloned.1.call-done = f32[16,128,128]{2,1,0:T(8,128)} async-done(((f32[16,1024,128]{2,1,0:T(8,128)}), f32[16,128,128]{2,1,0:T(8,128)}) %reduce-scatter.19.cloned.1.call-update) | async-done | bytes 1048592 | tf_op jit(solution)/shard_map/reduce_scatter | solution.py:388
  1365.1 151.2 %reduce-scatter.21.cloned.1.call-done = f32[16,128,128]{2,1,0:T(8,128)} async-done(((f32[16,1024,128]{2,1,0:T(8,128)}), f32[16,128,128]{2,1,0:T(8,128)}) %reduce-scatter.21.cloned.1.call-update) | async-done | bytes 1048592 | tf_op jit(solution)/shard_map/reduce_scatter | solution.py:389
  (298 shorter events, 35.6 us)
Async XLA Ops:
  7.2 30.4 %copy-start = (bf16[256,1024]{1,0:T(8,128)(2,1)S(1)}, bf16[256,1024]{1,0:T(8,128)(2,1)}, u32[]{:S(2)}) copy-start(bf16[256,1024]{1,0:T(8,128)(2,1)} %param.22) | copy-start | bytes 1572868
  7.2 5.7 copy-start.35
  7.2 144.5 %all-reduce.10.cloned.1.call-start = ((), (), s32[]{:S(2)}) async-start(), calls=%async_computation.8 | async-start | bytes 4194304 | tf_op jit(solution)/shard_map/psum | solution.py:191
  9.5 4.2 copy-start.49
  10.1 4.5 copy-start.68
  10.6 4.1 copy-start.27
  10.6 4.1 copy-start.29
  12.9 8.7 copy-start.5
  14.7 10.7 copy-start.31
  14.7 10.7 copy-start.33
  15.5 9.9 copy-start.41
  18.7 11.3 copy-start.25
  21.6 8.5 copy-start.64
  25.4 9.2 copy-start.23
  28.1 6.5 copy-start.10
  28.1 5.2 copy-start.13
  28.2 5.2 copy-start.37
  30.0 6.8 copy-start.60
  36.9 7.4 copy-start.51
  39.6 582.4 %all-reduce.12.cloned.1.call-start = ((), (), s32[]{:S(2)}) async-start(), calls=%async_computation.9 | async-start | bytes 4194304 | tf_op jit(solution)/shard_map/psum | solution.py:267
  56.4 6.8 copy-start.82
  56.4 7.0 copy-start.85
  62.2 32.4 %copy-start.54 = (s32[1024,8]{0,1:T(8,128)}, s32[1024,8]{0,1:T(8,128)S(1)}, u32[]{:S(2)}) copy-start(s32[1024,8]{0,1:T(8,128)S(1)} %get-tuple-element.114) | copy-start | bytes 98308
  62.2 139.1 %copy-start.62 = (pred[1024,8]{0,1:T(8,128)(4,1)}, pred[1024,8]{0,1:T(8,128)(4,1)S(1)}, u32[]{:S(2)}) copy-start(pred[1024,8]{0,1:T(8,128)(4,1)S(1)} %get-tuple-element.116) | copy-start | bytes 24580
  94.5 57.2 %copy-start.53 = (s32[1,10240]{1,0:T(1,128)}, s32[1,10240]{1,0:T(1,128)S(1)}, u32[]{:S(2)}) copy-start(s32[1,10240]{1,0:T(1,128)S(1)} %compare_select_fusion) | copy-start | bytes 122884
  101.0 6.6 copy-start.3
  155.5 44.9 %copy-start.70 = (f32[1024]{0:T(1024)}, f32[1024]{0:T(1024)S(1)}, u32[]{:S(2)}) copy-start(f32[1024]{0:T(1024)S(1)} %get-tuple-element.157) | copy-start | bytes 12292
  156.3 44.1 %copy-start.1 = (bf16[1024,1024]{1,0:T(8,128)(2,1)}, bf16[1024,1024]{1,0:T(8,128)(2,1)S(1)}, u32[]{:S(2)}) copy-start(bf16[1024,1024]{1,0:T(8,128)(2,1)S(1)} %multiply_convert_fusion.1) | copy-start | bytes 6291460
  156.3 44.1 %copy-start.73 = (bf16[1024,16]{0,1:T(8,128)(2,1)S(1)}, bf16[1024,16]{0,1:T(8,128)(2,1)}, u32[]{:S(2)}) copy-start(bf16[1024,16]{0,1:T(8,128)(2,1)} %param.25) | copy-start | bytes 98308
  201.2 50.6 %copy-start.66 = (f32[1024]{0:T(1024)}, f32[1024]{0:T(1024)S(1)}, u32[]{:S(2)}) copy-start(f32[1024]{0:T(1024)S(1)} %fusion.77) | copy-start | bytes 12292
  232.7 19.1 %copy-start.56 = (f32[10241]{0:T(1024)}, f32[10241]{0:T(1024)S(1)}, u32[]{:S(2)}) copy-start(f32[10241]{0:T(1024)S(1)} %scatter_custom_fusion) | copy-start | bytes 122896
  232.7 19.1 %copy-start.18 = (bf16[16,1024,128]{1,2,0:T(8,128)(2,1)S(1)}, bf16[16,1024,128]{1,2,0:T(8,128)(2,1)}, u32[]{:S(2)}) copy-start(bf16[16,1024,128]{1,2,0:T(8,128)(2,1)} %copy.130) | copy-start | bytes 12582916
  232.8 19.0 %copy-start.19 = (bf16[16,1024,128]{1,2,0:T(8,128)(2,1)S(1)}, bf16[16,1024,128]{1,2,0:T(8,128)(2,1)}, u32[]{:S(2)}) copy-start(bf16[16,1024,128]{1,2,0:T(8,128)(2,1)} %copy.131) | copy-start | bytes 12582916
  273.5 17.9 %slice-start.2 = ((f32[10241]{0:T(1024)}), f32[10240]{0:T(1024)S(1)}, s32[]{:S(2)}) async-start(f32[10241]{0:T(1024)} %copy-done.56), calls=%async_computation.21 | async-start | bytes 81920 | tf_op jit(solution)/shard_map/slice | solution.py:227
  348.5 19.6 %copy-start.20 = (bf16[1,16,640,128]{2,3,1,0:T(8,128)(2,1)}, bf16[1,16,640,128]{2,3,1,0:T(8,128)(2,1)S(1)}, u32[]{:S(2)}) copy-start(bf16[1,16,640,128]{2,3,1,0:T(8,128)(2,1)S(1)} %get-tuple-element.132) | copy-start | bytes 7864324
  462.8 276.1 %all-reduce.14.cloned.1.call-start = ((), (), s32[]{:S(2)}) async-start(), calls=%async_computation.18 | async-start | bytes 8388608 | tf_op jit(solution)/shard_map/psum | solution.py:237
  514.5 94.4 %copy-start.55 = (s32[1024,8]{0,1:T(8,128)S(1)}, s32[1024,8]{0,1:T(8,128)}, u32[]{:S(2)}) copy-start(s32[1024,8]{0,1:T(8,128)} %copy-done.54) | copy-start | bytes 98308
  514.5 94.4 %copy-start.63 = (pred[1024,8]{0,1:T(8,128)(4,1)S(1)}, pred[1024,8]{0,1:T(8,128)(4,1)}, u32[]{:S(2)}) copy-start(pred[1024,8]{0,1:T(8,128)(4,1)} %copy-done.62) | copy-start | bytes 24580
  514.5 107.4 %copy-start.40 = (f32[1024,8]{0,1:T(8,128)S(1)}, f32[1024,8]{0,1:T(8,128)}, u32[]{:S(2)}) copy-start(f32[1024,8]{0,1:T(8,128)} %copy-done.39) | copy-start | bytes 98308
  514.5 107.3 %copy-start.59 = (f32[1024]{0:T(1024)S(1)}, f32[1024]{0:T(1024)}, u32[]{:S(2)}) copy-start(f32[1024]{0:T(1024)} %copy-done.58) | copy-start | bytes 12292
  514.5 107.3 %copy-start.67 = (f32[1024]{0:T(1024)S(1)}, f32[1024]{0:T(1024)}, u32[]{:S(2)}) copy-start(f32[1024]{0:T(1024)} %copy-done.66) | copy-start | bytes 12292
  514.6 107.4 %copy-start.52 = (s32[1024,8]{0,1:T(8,128)S(1)}, s32[1024,8]{0,1:T(8,128)}, u32[]{:S(2)}) copy-start(s32[1024,8]{0,1:T(8,128)} %param.31) | copy-start | bytes 98308
  514.6 107.5 %copy-start.71 = (f32[1024]{0:T(1024)S(1)}, f32[1024]{0:T(1024)}, u32[]{:S(2)}) copy-start(f32[1024]{0:T(1024)} %copy-done.70) | copy-start | bytes 12292
  514.6 107.5 %copy-start.74 = (bf16[1024,16]{0,1:T(8,128)(2,1)S(1)}, bf16[1024,16]{0,1:T(8,128)(2,1)}, u32[]{:S(2)}) copy-start(bf16[1024,16]{0,1:T(8,128)(2,1)} %param.25) | copy-start | bytes 98308
  514.6 107.5 %copy-start.76 = (f32[1024]{0:T(1024)S(1)}, f32[1024]{0:T(1024)}, u32[]{:S(2)}) copy-start(f32[1024]{0:T(1024)} %param.24) | copy-start | bytes 12292
  622.0 4.2 copy-start.4
  622.0 4.2 copy-start.78
  622.1 4.1 copy-start.8
  622.1 4.7 copy-start.17
  628.4 5.0 copy-start.11
  629.3 4.2 copy-start.38
  643.8 7.0 copy-start.48
  652.9 144.5 %reduce-scatter.17.cloned.1.call-start = ((), (), s32[]{:S(2)}) async-start(), calls=%async_computation.14 | async-start | bytes 73728 | tf_op jit(solution)/shard_map/reduce_scatter | solution.py:387
  655.5 207.4 %reduce-scatter.13.cloned.1.call-start = ((), (), s32[]{:S(2)}) async-start(), calls=%async_computation.12 | async-start | bytes 589824 | tf_op jit(solution)/shard_map/reduce_scatter | solution.py:383
  658.8 269.4 %reduce-scatter.11.cloned.1.call-start = ((), (), s32[]{:S(2)}) async-start(), calls=%async_computation.11 | async-start | bytes 589824 | tf_op jit(solution)/shard_map/reduce_scatter | solution.py:382
  660.5 335.3 %reduce-scatter.15.cloned.1.call-start = ((), (), s32[]{:S(2)}) async-start(), calls=%async_computation.13 | async-start | bytes 1179648 | tf_op jit(solution)/shard_map/reduce_scatter | solution.py:384
  664.6 398.3 %reduce-scatter.9.cloned.1.call-start = ((), (), s32[]{:S(2)}) async-start(), calls=%async_computation.10 | async-start | bytes 1179648 | tf_op jit(solution)/shard_map/reduce_scatter | solution.py:381
  666.5 547.6 %reduce-scatter.23.cloned.1.call-start = ((), (), s32[]{:S(2)}) async-start(), calls=%async_computation.17 | async-start | bytes 9437184 | tf_op jit(solution)/shard_map/reduce_scatter | solution.py:390
  681.2 683.9 %reduce-scatter.19.cloned.1.call-start = ((), (), s32[]{:S(2)}) async-start(), calls=%async_computation.15 | async-start | bytes 9437184 | tf_op jit(solution)/shard_map/reduce_scatter | solution.py:388
  695.5 820.8 %reduce-scatter.21.cloned.1.call-start = ((), (), s32[]{:S(2)}) async-start(), calls=%async_computation.16 | async-start | bytes 9437184 | tf_op jit(solution)/shard_map/reduce_scatter | solution.py:389
  710.2 28.7 %copy-start.9 = (bf16[1024,1024]{1,0:T(8,128)(2,1)S(1)}, bf16[1024,1024]{1,0:T(8,128)(2,1)}, u32[]{:S(2)}) copy-start(bf16[1024,1024]{1,0:T(8,128)(2,1)} %param.18) | copy-start | bytes 6291460
  710.2 28.7 %copy-start.69 = (f32[1024]{0:T(1024)S(1)}, f32[1024]{0:T(1024)}, u32[]{:S(2)}) copy-start(f32[1024]{0:T(1024)} %copy-done.68) | copy-start | bytes 12292
  710.2 28.7 %copy-start.72 = (f32[1024]{0:T(1024)S(1)}, f32[1024]{0:T(1024)}, u32[]{:S(2)}) copy-start(f32[1024]{0:T(1024)} %param.23) | copy-start | bytes 12292
  710.3 54.7 %copy-start.77 = (f32[1024]{0:T(1024)S(1)}, f32[1024]{0:T(1024)}, u32[]{:S(2)}) copy-start(f32[1024]{0:T(1024)} %get-tuple-element.154) | copy-start | bytes 12292
  (38 other events, 88.2 us)
Sparse Core Ops, SparseCore 0:
  39.8 54.0 all-reduce.9
  462.9 54.0 all-reduce.11
  653.0 85.8 all-reduce.13
  742.4 54.9 reduce-scatter.16
  801.2 61.5 reduce-scatter.12
  866.6 61.5 reduce-scatter.10
  932.2 63.5 reduce-scatter.14
  999.8 63.0 reduce-scatter.8
  1067.2 146.8 reduce-scatter.22
  1218.1 146.9 reduce-scatter.18
  1369.3 146.9 reduce-scatter.20
where the time goes:
time: 1530 us; the launch traced here: 1520 us
  waiting for transfers between devices  772 us (50%)
  other arithmetic  285 us (19%)
  local copies, waits for them, and re-layouts  260 us (17%)
  matrix products  155 us (10%)
  blocking collectives  34.5 us (2%)
  between operations  16.6 us (1%)
    reduce_scatter x1, waiting for transfers between devices, body(): lax.psum_scatter(grad_up, 'dp', scatter_dimension=1, tiled=True)  151 us
    reduce_scatter x1, waiting for transfers between devices, body(): lax.psum_scatter(grad_down, 'dp', scatter_dimension=2, tiled=True)  151 us
    reduce_scatter x1, waiting for transfers between devices, body(): lax.psum_scatter(grad_gate, 'dp', scatter_dimension=1, tiled=True)  151 us
    scatter-add x1, other arithmetic, body(): jax.ops.segment_sum(grad_disp, token_table, num_segments=row_count + 1)  90.9 us
    scatter-add x1, other arithmetic, body(): jax.ops.segment_sum(gate_table[:, None] * expert_part, token_table, num_s...  90.5 us
    reduce_scatter x1, waiting for transfers between devices, body(): lax.psum_scatter(grad_output, 'dp', scatter_dimension=1, tiled=True)  67.6 us
    reduce_scatter x1, waiting for transfers between devices, body(): lax.psum_scatter(grad_query, 'dp', scatter_dimension=0, tiled=True)  67.1 us
    unnamed x189, local copies, waits for them, and re-layouts  66.2 us
  transfers between devices with their start and end apart: 11, of which 9 were waited for; matrix products, arithmetic and copies ran while one was open for 21% of the time, Pallas kernels for 0%

commit v1 on v0

v1 whole, which is shorter than its diff:
```python
import jax
import jax.numpy as jnp
from jax import lax
from jax.sharding import PartitionSpec as P

MODEL_WIDTH = 1024
HEAD_SIZE = 64
E = 16
PIECE = 256
QBLK = 512
CAP = 640

epsilon = 1e-06
negative = -1e30
F32 = jnp.float32
BF16 = jnp.bfloat16


def mm(left, right, dims):
    return lax.dot_general(left, right, (dims, ((), ())), preferred_element_type=F32)


def rope_tables(sequence_length):
    half_width = HEAD_SIZE // 2
    frequency = 10000.0 ** (-(jnp.arange(half_width, dtype=F32) * 2.0 / HEAD_SIZE))
    angles = jnp.arange(sequence_length, dtype=F32)[:, None] * frequency[None, :]
    return (jnp.cos(angles), jnp.sin(angles))


def apply_rotation(values, cosine_table, sine_values):
    half_width = HEAD_SIZE // 2
    first = values[..., :half_width]
    second = values[..., half_width:]
    cos_part = cosine_table[:, None, :]
    sin_part = sine_values[:, None, :]
    return jnp.concatenate(
        [first * cos_part - second * sin_part, second * cos_part + first * sin_part], axis=-1
    )


def unrotate(grads, cosine_table, sine_values):
    return apply_rotation(grads, cosine_table, -sine_values)


def allowed(starts, kind_row, row_pos, col_pos):
    ends = starts + PIECE
    inside_row = (
        (kind_row[None, :] == 1)
        & (row_pos[:, None] >= starts[None, :])
        & (row_pos[:, None] < ends[None, :])
    )
    inside_col = (
        (kind_row[None, :] == 1)
        & (col_pos[:, None] >= starts[None, :])
        & (col_pos[:, None] < ends[None, :])
    )
    same_piece = jnp.any(inside_row[:, None, :] & inside_col[None, :, :], axis=-1)
    return (col_pos[None, :] <= row_pos[:, None]) | same_piece


CORE_PAIRS = [(i, i ^ 1) for i in range(4)]
X_PAIRS = [(i, i ^ 2) for i in range(4)]


def reduce_half(part, core):
    half = part.shape[0] // 2
    mine = lax.dynamic_slice_in_dim(part, core * half, half, 0)
    other = lax.dynamic_slice_in_dim(part, (1 - core) * half, half, 0)
    got = lax.ppermute(other, "tensor", CORE_PAIRS)
    total = (mine.astype(F32) + got.astype(F32)).astype(part.dtype)
    far = lax.ppermute(total, "tensor", X_PAIRS)
    return total.astype(F32) + far.astype(F32)


def share_half(half_rows, core):
    got = lax.ppermute(half_rows, "tensor", CORE_PAIRS)
    pair = jnp.stack([jnp.where(core == 0, half_rows, got), jnp.where(core == 0, got, half_rows)])
    return pair.reshape((2 * half_rows.shape[0],) + half_rows.shape[1:])


def scatter_sum(blocks, ways):
    me = lax.axis_index("dp")
    if ways != 8:
        return lax.psum_scatter(blocks, "dp", scatter_dimension=0, tiled=False).astype(F32)
    y = me % 2
    z = me // 2
    grid = blocks.reshape((4, 2) + blocks.shape[1:])
    mine = lax.dynamic_index_in_dim(grid, y, 1, keepdims=False)
    other = lax.dynamic_index_in_dim(grid, 1 - y, 1, keepdims=False)
    got = lax.ppermute(other, "dp", [(i, i ^ 1) for i in range(8)])
    summed = (mine.astype(F32) + got.astype(F32)).astype(blocks.dtype)
    total = lax.dynamic_index_in_dim(summed, z, 0, keepdims=False).astype(F32)
    for step in (1, 2, 3):
        block = lax.dynamic_index_in_dim(summed, (z + step) % 4, 0, keepdims=False)
        arrived = lax.ppermute(
            block, "dp", [(i, (i + 2 * step) % 8) for i in range(8)]
        )
        total = total + arrived.astype(F32)
    return total


def make_body(ways):
    def body(
        tokens,
        w_query,
        key_weight,
        value_weight,
        w_output,
        gain_attn,
        gain_ffn,
        router,
        w_gate,
        w_up,
        w_down,
        piece_start,
        piece_kind,
        choices,
        place_order,
        cotangent,
    ):
        rows = tokens.shape[0]
        half = rows // 2
        width = tokens.shape[1]
        kv_local = key_weight.shape[1] // HEAD_SIZE
        q_local = w_query.shape[1] // HEAD_SIZE
        ff = w_gate.shape[2]
        group = q_local // kv_local
        scale = HEAD_SIZE ** (-0.5)
        core = lax.axis_index("tensor") % 2

        def my_half(array):
            return lax.dynamic_slice_in_dim(array, core * half, half, 0)

        resid_in = tokens.astype(F32)
        inv_one = lax.rsqrt(jnp.mean(resid_in * resid_in, axis=1, keepdims=True) + epsilon)
        first_normed = (resid_in * inv_one * gain_attn).astype(BF16)
        cos_rows, sin_rows = rope_tables(rows)
        qp = mm(first_normed, w_query, ((1,), (0,))).reshape(rows, q_local, HEAD_SIZE)
        q = apply_rotation(qp, cos_rows, sin_rows).astype(BF16)
        q = q.reshape(rows, kv_local, group, HEAD_SIZE)
        kp = mm(first_normed, key_weight, ((1,), (0,))).reshape(rows, kv_local, HEAD_SIZE)
        k = apply_rotation(kp, cos_rows, sin_rows).astype(BF16)
        v = mm(first_normed, value_weight, ((1,), (0,))).astype(BF16)
        v = v.reshape(rows, kv_local, HEAD_SIZE)
        blocks = rows // QBLK

        def block_scores(block):
            start = block * QBLK
            length = start + QBLK
            scores = (
                jnp.einsum(
                    "qgrd,kgd->grqk", q[start:length], k[:length], preferred_element_type=F32
                )
                * scale
            )
            visible = allowed(
                piece_start[0],
                piece_kind[0],
                start + jnp.arange(QBLK, dtype=jnp.int32),
                jnp.arange(length, dtype=jnp.int32),
            )
            return jnp.where(visible[None, None], scores, negative)

        outs, totals = [], []
        for block in range(blocks):
            scores = block_scores(block)
            top = jnp.max(scores, axis=-1, keepdims=True)
            total = top + jnp.log(jnp.sum(jnp.exp(scores - top), axis=-1, keepdims=True))
            probs = jnp.exp(scores - total).astype(BF16)
            length = (block + 1) * QBLK
            res = jnp.einsum("grqk,kgd->qgrd", probs, v[:length], preferred_element_type=F32)
            outs.append(res.astype(BF16))
            totals.append(total)
        head_out = jnp.concatenate(outs, axis=0).reshape(rows, q_local * HEAD_SIZE)
        attn_part = mm(head_out, w_output, ((1,), (0,))).astype(BF16)
        mid = my_half(resid_in) + reduce_half(attn_part, core)
        inv_two = lax.rsqrt(jnp.mean(mid * mid, axis=1, keepdims=True) + epsilon)
        normed_half = (mid * inv_two * gain_ffn).astype(BF16)
        normed = share_half(normed_half, core)

        expert_ids = jnp.arange(E, dtype=jnp.int32)
        picked = jnp.any(choices[:, :, None] == expert_ids[None, None, :], axis=1)
        ranks = place_order[0]
        earlier = (ranks[None, :] < ranks[:, None]).astype(BF16)
        slot = mm(earlier, picked.astype(BF16), ((1,), (0,)))
        kept = (picked & (slot < CAP)).astype(F32)
        logits = mm(normed, router, ((1,), (0,)))
        logits = jnp.where(picked, logits, negative)
        gates = jax.nn.softmax(logits, axis=1)
        gates = jnp.where(picked, gates, 0.0)
        slot_gate = gates * kept

        gate_pre = jnp.einsum("td,edf->tef", normed, w_gate, preferred_element_type=F32)
        up_pre = jnp.einsum("td,edf->tef", normed, w_up, preferred_element_type=F32)
        dy_down = jnp.einsum("td,efd->tef", cotangent, w_down, preferred_element_type=F32)
        sigmoid = jax.nn.sigmoid(gate_pre)
        act = gate_pre * sigmoid
        hidden = act * up_pre
        gated = (slot_gate[:, :, None] * hidden).astype(BF16)
        grad_gate_part = jnp.sum(hidden * dy_down, axis=2) * kept
        grad_hidden = slot_gate[:, :, None] * dy_down
        slope = sigmoid * (1.0 + gate_pre * (1.0 - sigmoid))
        grad_a = (grad_hidden * up_pre * slope).astype(BF16)
        grad_u = (grad_hidden * act).astype(BF16)
        moe_part = jnp.einsum("tef,efd->td", gated, w_down, preferred_element_type=F32)
        norm_part = jnp.einsum("tef,edf->td", grad_a, w_gate, preferred_element_type=F32)
        norm_part = norm_part + jnp.einsum("tef,edf->td", grad_u, w_up, preferred_element_type=F32)
        piece = width // ways
        grad_gate = jnp.einsum("td,tef->edf", normed, grad_a, preferred_element_type=F32)
        grad_up = jnp.einsum("td,tef->edf", normed, grad_u, preferred_element_type=F32)
        grad_down = jnp.einsum("tef,td->efd", gated, cotangent, preferred_element_type=F32)

        def send_rows(grad):
            e, d, f = grad.shape
            return grad.astype(BF16).reshape(e, ways, d // ways, f).transpose(1, 0, 2, 3)

        def send_columns(grad):
            e, f, d = grad.shape
            return grad.astype(BF16).reshape(e, f, ways, d // ways).transpose(2, 0, 1, 3)

        sent_gate = scatter_sum(send_rows(grad_gate), ways)
        sent_up = scatter_sum(send_rows(grad_up), ways)
        sent_down = scatter_sum(send_columns(grad_down), ways)

        norm_half = reduce_half(norm_part.astype(BF16), core)
        dg_half = reduce_half(grad_gate_part, core)
        output = share_half(
            (mid + reduce_half(moe_part.astype(BF16), core)).astype(BF16), core
        )
        gates_half = my_half(gates)
        dz = gates_half * (dg_half - jnp.sum(gates_half * dg_half, axis=1, keepdims=True))
        dlg = dz.astype(BF16)
        grad_norm = norm_half + mm(dlg, router, ((1,), (1,)))
        grad_router = mm(dlg, normed_half, ((0,), (0,)))
        grad_gain_ffn = jnp.sum(grad_norm * mid * inv_two, axis=0)
        scaled = gain_ffn * grad_norm
        grad_mid = (
            my_half(cotangent).astype(F32)
            + inv_two * scaled
            - mid * inv_two**3 * jnp.mean(scaled * mid, axis=1, keepdims=True)
        )
        grad_attn = share_half(grad_mid.astype(BF16), core)
        grad_output = mm(head_out, grad_attn, ((0,), (0,)))
        sent_output = scatter_sum(
            grad_output.astype(BF16).reshape(q_local * HEAD_SIZE, ways, piece).transpose(1, 0, 2),
            ways,
        )
        grad_heads = mm(grad_attn, w_output, ((1,), (1,))).astype(BF16)
        grad_heads = grad_heads.reshape(rows, kv_local, group, HEAD_SIZE)
        query_parts = []
        grad_k = jnp.zeros((rows, kv_local, HEAD_SIZE), F32)
        grad_v = jnp.zeros((rows, kv_local, HEAD_SIZE), F32)
        for block in range(blocks):
            scores = block_scores(block)
            start = block * QBLK
            length = start + QBLK
            probs = jnp.exp(scores - totals[block])
            dob = grad_heads[start:length]
            dp = jnp.einsum("qgrd,kgd->grqk", dob, v[:length], preferred_element_type=F32)
            delta = jnp.sum(probs * dp, axis=-1, keepdims=True)
            ds = (probs * (dp - delta)).astype(BF16)
            query_parts.append(
                jnp.einsum("grqk,kgd->qgrd", ds, k[:length], preferred_element_type=F32) * scale
            )
            dk = jnp.einsum("grqk,qgrd->kgd", ds, q[start:length], preferred_element_type=F32)
            dv = jnp.einsum("grqk,qgrd->kgd", probs.astype(BF16), dob, preferred_element_type=F32)
            pad = ((0, rows - length), (0, 0), (0, 0))
            grad_k = grad_k + jnp.pad(dk * scale, pad)
            grad_v = grad_v + jnp.pad(dv, pad)
        grad_q = jnp.concatenate(query_parts, axis=0).reshape(rows, q_local, HEAD_SIZE)
        dqp = unrotate(grad_q, cos_rows, sin_rows).astype(BF16).reshape(rows, -1)
        dkp = unrotate(grad_k, cos_rows, sin_rows).astype(BF16).reshape(rows, -1)
        dvb = grad_v.astype(BF16).reshape(rows, -1)
        grad_qkv = jnp.concatenate([dqp, dkp, dvb], axis=1)
        w_qkv = jnp.concatenate([w_query, key_weight, value_weight], axis=1)
        grad_wide = mm(first_normed, grad_qkv, ((0,), (0,))).astype(BF16)
        sent_qkv = scatter_sum(grad_wide.reshape(ways, piece, -1), ways)
        nq, nk = w_query.shape[1], key_weight.shape[1]
        normed_one_part = mm(grad_qkv, w_qkv, ((1,), (1,)))
        norm_one_half = reduce_half(normed_one_part.astype(BF16), core)
        x_half = my_half(resid_in)
        inv_half = my_half(inv_one)
        grad_gain_attn = jnp.sum(norm_one_half * x_half * inv_half, axis=0)
        scaled_one = gain_attn * norm_one_half
        input_half = (
            grad_mid
            + inv_half * scaled_one
            - x_half * inv_half**3 * jnp.mean(scaled_one * x_half, axis=1, keepdims=True)
        ).astype(BF16)
        input_grad = share_half(input_half, core)
        small = jnp.concatenate([grad_gain_attn[None], grad_gain_ffn[None], grad_router], axis=0)
        small = small + lax.ppermute(small, "tensor", CORE_PAIRS)
        count = small.shape[0]
        small = scatter_sum(small.reshape(count, ways, piece).transpose(1, 0, 2), ways)
        return (
            output,
            input_grad,
            sent_qkv[:, :nq],
            sent_qkv[:, nq : nq + nk],
            sent_qkv[:, nq + nk :],
            sent_output,
            small[0],
            small[1],
            small[2:].T,
            sent_gate,
            sent_up,
            sent_down,
        )

    return body


def solution(mesh):
    return jax.shard_map(
        make_body(mesh.shape["dp"]),
        mesh=mesh,
        in_specs=(
            P("dp", None),
            P(None, "tensor"),
            P(None, "tensor"),
            P(None, "tensor"),
            P("tensor", None),
            P(),
            P(),
            P(),
            P(None, None, "tensor"),
            P(None, None, "tensor"),
            P(None, "tensor", None),
            P("dp", None),
            P("dp", None),
            P("dp", None),
            P("dp", None),
            P("dp", None),
        ),
        out_specs=(
            P("dp", None),
            P("dp", None),
            P("dp", "tensor"),
            P("dp", "tensor"),
            P("dp", "tensor"),
            P("tensor", "dp"),
            P("dp"),
            P("dp"),
            P("dp", None),
            P(None, "dp", "tensor"),
            P(None, "dp", "tensor"),
            P(None, "tensor", "dp"),
        ),
        check_vma=False,
    )
```

time: 1530 us -> 457 us (0.30)
  waiting for transfers between devices: 772 us -> 117 us
  other arithmetic: 285 us -> 45.5 us
  local copies, waits for them, and re-layouts: 260 us -> 57.9 us
  starting transfers between devices: 0.46 us -> 112 us
  matrix products: 155 us -> 116 us
  blocking collectives: 34.5 us -> 0 us
    reduce_scatter x8 -> x0, waiting for transfers between devices: 745 us -> none  [the longest x1 151 us: body(): lax.psum_scatter(grad_up, 'dp', scatter_dimension=1, tiled=True)]
    scatter-add x2 -> x0, other arithmetic: 181 us -> none  [the longest x1 90.9 us: body(): jax.ops.segment_sum(grad_disp, token_table, num_segments=row_count + 1)]
    gather x9 -> x0, local copies, waits for them, and re-layouts: 150 us -> none  [the longest x3 51.1 us: body(): jnp.take(slot_dot, global_flat, axis=0, mode='fill', fill_value=0)]
    ppermute x0 -> x39, waiting for transfers between devices: none -> 117 us  [the longest x6 61.6 us: scatter_sum(): got = lax.ppermute(other, 'dp', [(i, i ^ 1) for i in range(8)])]
    ppermute x0 -> x39, starting transfers between devices: none -> 112 us  [the longest x18 94.3 us: scatter_sum(): lax.ppermute(block, 'dp', [(i, (i + 2 * step) % 8) for i in range(8)])]
    dot_general x34 -> x31, matrix products: 155 us -> 102 us  [the longest x1 25.4 us: body(): jnp.einsum('td,efd->tef', cotangent, w_down, preferred_element_type=F32)]
    reduce_sum x10 -> x6, other arithmetic: 50 us -> 4.21 us  [the longest x2 2.93 us: body(): jnp.sum(jnp.exp(scores - top), axis=-1, keepdims=True)]
    unnamed x189 -> x147, local copies, waits for them, and re-layouts: 66.2 us -> 26.7 us
  transfers between devices with their start and end apart: 11 -> 39, of which waited for: 9 -> 15; matrix products, arithmetic and copies ran while one was open for 21% -> 25% of each run, Pallas kernels for 0% -> 0%
where the time goes in v1:
time: 457 us; the launch traced here: 451 us
  waiting for transfers between devices  117 us (26%)
  matrix products  116 us (25%)
  starting transfers between devices  112 us (25%)
  local copies, waits for them, and re-layouts  57.9 us (13%)
  other arithmetic  45.5 us (10%)
    ppermute x18, starting transfers between devices, scatter_sum(): lax.ppermute(block, 'dp', [(i, (i + 2 * step) % 8) for i in range(8)])  94.3 us
    ppermute x6, waiting for transfers between devices, scatter_sum(): got = lax.ppermute(other, 'dp', [(i, i ^ 1) for i in range(8)])  61.6 us
    unnamed x147, local copies, waits for them, and re-layouts  26.7 us
    ppermute x18, waiting for transfers between devices, scatter_sum(): lax.ppermute(block, 'dp', [(i, (i + 2 * step) % 8) for i in range(8)])  26.5 us
    dot_general x1, matrix products, body(): jnp.einsum('td,efd->tef', cotangent, w_down, preferred_element_type=F32)  25.4 us
    ppermute x5, waiting for transfers between devices, reduce_half(): far = lax.ppermute(total, 'tensor', X_PAIRS)  25.2 us
    dot_general x12, matrix products, mm(): lax.dot_general(left, right, (dims, ((), ())), preferred_element_type=F32)  15.5 us
    unnamed x2, matrix products  13.9 us
  transfers between devices with their start and end apart: 39, of which 15 were waited for; matrix products, arithmetic and copies ran while one was open for 25% of the time, Pallas kernels for 0%

profile of v1, /device:TPU:0, one launch (start us, length us, event | category | flops | bytes accessed | tf_op | source)
XLA Modules:
  0.0 450.9 jit_solution(14798972857075017135)
XLA Ops:
  1.9 2.1 multiply_reduce_fusion.1
  4.1 2.6 fusion.93
  10.6 1.8 copy.68
  12.4 2.0 fusion.58
  14.4 1.6 fusion.5
  16.1 2.0 exponential_reduce_fusion
  19.5 1.6 convolution_convert_fusion.9
  23.6 2.0 fusion.16
  25.6 1.9 copy-done.2
  28.5 5.8 %fusion.32 = bf16[512,2,2,64]{0,3,2,1:T(8,128)(2,1)S(1)} fusion(bf16[1024,2,64,1]{0,2,3,1:T(8,128)(2,1)} %bitcast.412, f32[2,1024,512,2]{2,1,3,0:T(8,128)} %copy-done.1, f32[2,2,512]{2,1,0:T(2,128)S(1)} %log_add_fusion, pred[512,1024]{0,1:T(8,128)(4,1)S(1)} %copy.68), kind=kOutput, calls=%fused_computation.96 | convolution fusion | flops 276955136 | bytes 9445376 | tf_op jit(solution)/shard_map/grqk,kgd->qgrd/dot_general | solution.py:171
  36.5 2.1 convolution_convert_fusion.3
  38.5 2.3 constant_dynamic-slice_fusion.10
  41.3 2.6 collective-permute-done
  43.9 1.9 add_convert_fusion.4
  45.9 2.9 collective-permute-start.1
  49.3 23.0 %collective-permute-done.1 = bf16[512,1024]{1,0:T(8,128)(2,1)S(1)} collective-permute-done((bf16[512,1024]{1,0:T(8,128)(2,1)S(1)}, bf16[512,1024]{1,0:T(8,128)(2,1)S(1)}, u32[]{:S(2)}, u32[]{:S(2)}) %collective-permute-start.1) | collective-permute-done | bytes 1048608 | tf_op jit(solution)/shard_map/ppermute | solution.py:71
  74.0 6.5 %copy.70 = bf16[16,1024,128]{1,2,0:T(8,128)(2,1)} copy(bf16[16,1024,128]{2,1,0:T(8,128)(2,1)} %param.24) | data formatting | bytes 8388608 | tf_op args[8]
  80.5 6.4 %copy.71 = bf16[16,1024,128]{1,2,0:T(8,128)(2,1)} copy(bf16[16,1024,128]{2,1,0:T(8,128)(2,1)} %param.25) | data formatting | bytes 8388608 | tf_op args[9]
  87.6 1.9 select_bitcast_fusion.7
  90.1 7.1 %fusion.99 = f32[1024,2048]{0,1} fusion(bf16[1024,1024]{1,0:T(8,128)(2,1)S(1)} %bitcast.383, bf16[1024,2048]{0,1:T(8,128)(2,1)S(1)} %bitcast.390), kind=kOutput, calls=%fused_computation.248 | convolution fusion | flops 4294967296 | bytes 14680064
  97.3 6.8 %fusion.100 = f32[1024,2048]{0,1} fusion(bf16[1024,1024]{1,0:T(8,128)(2,1)S(1)} %bitcast.384, bf16[1024,2048]{0,1:T(8,128)(2,1)S(1)} %bitcast.389), kind=kOutput, calls=%fused_computation.249 | convolution fusion | flops 4294967296 | bytes 14680064
  105.6 25.4 %multiply_convert_fusion = (bf16[1024,16,128]{0,2,1:T(8,128)(2,1)}, f32[1024,16]{0,1:T(8,128)S(1)}, bf16[1024,16,128]{0,2,1:T(8,128)(2,1)}, bf16[1024,16,128]{0,2,1:T(8,128)(2,1)}) fusion(f32[1024,16]{0,1:T(8,128)S(1)} %get-tuple-element.20, f32[1024,2048]{0,1} %fusion.99, f32[1024,2048]{0,1} %fusion.100, f32[1024,16,128]{0,2,1:T(8,128)} %bitcast.435, ...), kind=kOutput, calls=%fused_computation.7 | convolution fusion | flops 4345282560 | bytes 52559872 | tf_op jit(solution)/shard_map/td,efd->tef/dot_general | solution.py:195
  131.0 7.5 %convert_bitcast_fusion = bf16[16,16,8,8,128]{4,3,2,1,0:T(8,128)(2,1)S(1)} fusion(bf16[1024,16,128]{0,2,1:T(8,128)(2,1)} %get-tuple-element.28, bf16[1024,1024]{1,0:T(8,128)(2,1)} %param.31), kind=kOutput, calls=%fused_computation.32 | convolution fusion | flops 4297064448 | bytes 10485760 | tf_op jit(solution)/shard_map/tef,td->efd/dot_general | solution.py:211
  138.6 5.7 %bitcast_convert_fusion = bf16[1024,1024]{1,0:T(8,128)(2,1)} fusion(bf16[1024,16,128]{0,2,1:T(8,128)(2,1)S(1)} %copy-done.66, bf16[16,128,1024]{2,1,0:T(8,128)(2,1)S(1)} %copy-done.58), kind=kOutput, calls=%fused_computation.30 | convolution fusion | flops 4296015872 | bytes 10485760 | tf_op jit(solution)/shard_map/tef,efd->td/dot_general | solution.py:205
  147.1 1.8 collective-permute-start.35
  150.2 6.1 %fusion.101 = f32[1024,1024,1]{1,0,2:T(8,128)} fusion(bf16[1024,16,128]{0,2,1:T(8,128)(2,1)S(1)} %copy-done.67, bf16[16,1024,128]{2,1,0:T(8,128)(2,1)S(1)} %copy-done.19), kind=kOutput, calls=%fused_computation.250 | convolution fusion | flops 4294967296 | bytes 12582912 | tf_op jit(solution)/shard_map/tef,edf->td/dot_general | solution.py:206
  156.4 6.1 %convolution_convert_fusion.1 = bf16[16,128,1024]{2,1,0:T(8,128)(2,1)} fusion(bf16[1024,16,128]{0,2,1:T(8,128)(2,1)S(1)} %copy-done.67, bf16[1024,1024,1]{1,0,2:T(8,128)(2,1)S(1)} %bitcast.386), kind=kOutput, calls=%fused_computation.42 | convolution fusion | flops 4297064448 | bytes 10485760 | tf_op jit(solution)/shard_map/td,tef->edf/dot_general | solution.py:209
  162.5 4.7 %convolution_convert_fusion = bf16[16,128,1024]{2,1,0:T(8,128)(2,1)S(1)} fusion(bf16[1024,16,128]{0,2,1:T(8,128)(2,1)S(1)} %copy-done.68, bf16[1024,1024,1]{1,0,2:T(8,128)(2,1)S(1)} %bitcast.387), kind=kOutput, calls=%fused_computation.41 | convolution fusion | flops 4297064448 | bytes 10485760 | tf_op jit(solution)/shard_map/td,tef->edf/dot_general | solution.py:210
  167.2 3.1 copy.112
  170.3 6.6 %copy.86 = bf16[16,8,128,128]{3,2,0,1:T(8,128)(2,1)} copy(bf16[16,8,128,128]{2,1,3,0:T(8,128)(2,1)} %bitcast.381) | data formatting | bytes 8388608 | tf_op jit(solution)/shard_map/reshape | solution.py:215
  176.9 3.3 dynamic-slice_bitcast_fusion.1
  180.2 1.8 collective-permute-start.31
  182.0 3.1 copy.111
  185.0 7.1 %copy.85 = bf16[16,8,128,128]{3,2,0,1:T(8,128)(2,1)} copy(bf16[16,8,128,128]{2,1,3,0:T(8,128)(2,1)} %bitcast.382) | data formatting | bytes 8388608 | tf_op jit(solution)/shard_map/reshape | solution.py:215
  194.1 9.4 %fusion.12 = bf16[1024,1024]{1,0:T(8,128)(2,1)S(1)} fusion(f32[1024,1024,1]{1,0,2:T(8,128)} %fusion.101, bf16[1024,16,128]{0,2,1:T(8,128)(2,1)} %get-tuple-element.26, bf16[16,1024,128]{2,1,0:T(8,128)(2,1)} %param.25), kind=kOutput, calls=%fused_computation.29 | convolution fusion | flops 4297064448 | bytes 14680064 | tf_op jit(solution)/shard_map/tef,edf->td/dot_general | solution.py:207
  205.6 2.2 collective-permute-done.9
  210.1 1.8 collective-permute-start.7
  212.7 2.6 fusion.6
  216.4 1.9 collective-permute-start.36
  218.2 22.6 %collective-permute-done.31 = bf16[4,16,128,128]{3,2,1,0:T(8,128)(2,1)} collective-permute-done((bf16[4,16,128,128]{3,2,1,0:T(8,128)(2,1)}, bf16[4,16,128,128]{3,2,1,0:T(8,128)(2,1)}, u32[]{:S(2)}, u32[]{:S(2)}) %collective-permute-start.31) | collective-permute-done | bytes 2097184 | tf_op jit(solution)/shard_map/ppermute | solution.py:90
  240.8 2.8 collective-permute-start.37
  243.7 2.4 fusion.7
  248.6 36.6 %collective-permute-done.27 = bf16[4,16,128,128]{3,2,1,0:T(8,128)(2,1)S(1)} collective-permute-done((bf16[4,16,128,128]{3,2,1,0:T(8,128)(2,1)S(1)}, bf16[4,16,128,128]{3,2,1,0:T(8,128)(2,1)S(1)}, u32[]{:S(2)}, u32[]{:S(2)}) %collective-permute-start.27) | collective-permute-done | bytes 2097184 | tf_op jit(solution)/shard_map/ppermute | solution.py:90
  285.2 1.8 collective-permute-start.32
  287.0 2.6 collective-permute-start.33
  293.9 8.2 %collective-permute-done.32 = bf16[16,128,128]{2,1,0:T(8,128)(2,1)} collective-permute-done((bf16[16,128,128]{2,1,0:T(8,128)(2,1)S(1)}, bf16[16,128,128]{2,1,0:T(8,128)(2,1)}, u32[]{:S(2)}, u32[]{:S(2)}) %collective-permute-start.32) | collective-permute-done | bytes 524320 | tf_op jit(solution)/shard_map/ppermute | solution.py:95
  302.1 23.4 %collective-permute-start.29 = (bf16[16,128,128]{2,1,0:T(8,128)(2,1)S(1)}, bf16[16,128,128]{2,1,0:T(8,128)(2,1)S(1)}, u32[]{:S(2)}, u32[]{:S(2)}) collective-permute-start(bf16[16,128,128]{2,1,0:T(8,128)(2,1)S(1)} %get-tuple-element.38), channel_id=1, source_target_pairs={{0,16},{4,20},{8,24},{12,28},{16,0},{20,4},{24,8},{28,12},{1,17},{... | collective-permute-start | bytes 1572872 | tf_op jit(solution)/shard_map/ppermute | solution.py:95
  325.5 29.1 %collective-permute-start.30 = (bf16[16,128,128]{2,1,0:T(8,128)(2,1)S(1)}, bf16[16,128,128]{2,1,0:T(8,128)(2,1)S(1)}, u32[]{:S(2)}, u32[]{:S(2)}) collective-permute-start(bf16[16,128,128]{2,1,0:T(8,128)(2,1)S(1)} %get-tuple-element.37), channel_id=1, source_target_pairs={{0,24},{4,28},{8,0},{12,4},{16,8},{20,12},{24,16},{28,20},{1,25},{... | collective-permute-start | bytes 1572872 | tf_op jit(solution)/shard_map/ppermute | solution.py:95
  354.6 2.6 fusion.48
  357.3 2.5 fusion.50
  359.7 8.6 %collective-permute-done.29 = bf16[16,128,128]{2,1,0:T(8,128)(2,1)S(1)} collective-permute-done((bf16[16,128,128]{2,1,0:T(8,128)(2,1)S(1)}, bf16[16,128,128]{2,1,0:T(8,128)(2,1)S(1)}, u32[]{:S(2)}, u32[]{:S(2)}) %collective-permute-start.29) | collective-permute-done | bytes 524320 | tf_op jit(solution)/shard_map/ppermute | solution.py:95
  368.4 1.7 collective-permute-done.30
  379.4 2.8 fusion
  382.2 2.8 fusion.2
  387.7 2.4 fusion.31
  394.2 1.6 convolution_convert_fusion.4
  402.0 10.1 %collective-permute-start.19 = (bf16[256,128]{1,0:T(8,128)(2,1)S(1)}, bf16[256,128]{1,0:T(8,128)(2,1)S(1)}, u32[]{:S(2)}, u32[]{:S(2)}) collective-permute-start(bf16[256,128]{1,0:T(8,128)(2,1)S(1)} %get-tuple-element.63), channel_id=1, source_target_pairs={{0,8},{4,12},{8,16},{12,20},{16,24},{20,28},{24,0},{28,4},{1,9},{5... | collective-permute-start | bytes 196616 | tf_op jit(solution)/shard_map/ppermute | solution.py:95
  412.0 1.6 collective-permute-start.20
  414.7 8.2 %collective-permute-start.15 = (bf16[128,512]{1,0:T(8,128)(2,1)S(1)}, bf16[128,512]{1,0:T(8,128)(2,1)S(1)}, u32[]{:S(2)}, u32[]{:S(2)}) collective-permute-start(bf16[128,512]{1,0:T(8,128)(2,1)S(1)} %get-tuple-element.56), channel_id=1, source_target_pairs={{0,8},{4,12},{8,16},{12,20},{16,24},{20,28},{24,0},{28,4},{1,9},{5... | collective-permute-start | bytes 393224 | tf_op jit(solution)/shard_map/ppermute | solution.py:95
  422.9 1.6 collective-permute-start.16
  426.2 2.1 collective-permute-done.15
  428.3 4.6 %collective-permute-done.16 = bf16[128,512]{1,0:T(8,128)(2,1)S(1)} collective-permute-done((bf16[128,512]{1,0:T(8,128)(2,1)S(1)}, bf16[128,512]{1,0:T(8,128)(2,1)S(1)}, u32[]{:S(2)}, u32[]{:S(2)}) %collective-permute-start.16) | collective-permute-done | bytes 131104 | tf_op jit(solution)/shard_map/ppermute | solution.py:95
  437.7 1.8 collective-permute-done.23
  439.5 3.3 collective-permute-start.24
  (297 shorter events, 73.7 us)
Async XLA Ops:
  0.6 35.8 %copy-start = (bf16[256,1024]{1,0:T(8,128)(2,1)S(1)}, bf16[256,1024]{1,0:T(8,128)(2,1)}, u32[]{:S(2)}) copy-start(bf16[256,1024]{1,0:T(8,128)(2,1)} %param.20) | copy-start | bytes 1572868
  1.9 6.7 %copy-start.23 = (f32[1024,32]{0,1:T(8,128)}, f32[1024,32]{0,1:T(8,128)S(1)}, u32[]{:S(2)}) copy-start(f32[1024,32]{0,1:T(8,128)S(1)} %get-tuple-element.81) | copy-start | bytes 393220
  8.7 7.4 %copy-start.29 = (bf16[1024,2,32]{0,2,1:T(8,128)(2,1)}, bf16[1024,2,32]{0,2,1:T(8,128)(2,1)S(1)}, u32[]{:S(2)}) copy-start(bf16[1024,2,32]{0,2,1:T(8,128)(2,1)S(1)} %get-tuple-element.55) | copy-start | bytes 393220
  8.7 14.8 %copy-start.27 = (bf16[1024,2,32]{0,2,1:T(8,128)(2,1)}, bf16[1024,2,32]{0,2,1:T(8,128)(2,1)S(1)}, u32[]{:S(2)}) copy-start(bf16[1024,2,32]{0,2,1:T(8,128)(2,1)S(1)} %get-tuple-element.54) | copy-start | bytes 393220
  12.4 16.1 %copy-start.11 = (pred[512,1024]{0,1:T(8,128)(4,1)}, pred[512,1024]{0,1:T(8,128)(4,1)S(1)}, u32[]{:S(2)}) copy-start(pred[512,1024]{0,1:T(8,128)(4,1)S(1)} %copy.68) | copy-start | bytes 1572868
  19.5 9.0 %copy-start.42 = (f32[2,2,512]{2,1,0:T(2,128)}, f32[2,2,512]{2,1,0:T(2,128)S(1)}, u32[]{:S(2)}) copy-start(f32[2,2,512]{2,1,0:T(2,128)S(1)} %log_add_fusion) | copy-start | bytes 24580
  23.5 10.8 %copy-start.13 = (pred[512,512]{0,1:T(8,128)(4,1)}, pred[512,512]{0,1:T(8,128)(4,1)S(1)}, u32[]{:S(2)}) copy-start(pred[512,512]{0,1:T(8,128)(4,1)S(1)} %copy.66) | copy-start | bytes 786436
  40.8 3.1 collective-permute-start
  45.9 26.4 %collective-permute-start.1 = (bf16[512,1024]{1,0:T(8,128)(2,1)S(1)}, bf16[512,1024]{1,0:T(8,128)(2,1)S(1)}, u32[]{:S(2)}, u32[]{:S(2)}) collective-permute-start(bf16[512,1024]{1,0:T(8,128)(2,1)S(1)} %add_convert_fusion.4), channel_id=1, source_target_pairs={{0,2},{1,3},{2,0},{3,1},{4,6},{5,7},{6,4},{7,5},{8,10},{9,11},{10,... | collective-permute-start | bytes 3145736 | tf_op jit(solution)/shard_map/ppermute | solution.py:71
  49.2 24.7 %copy-start.5 = (f32[1024,1024]{1,0:T(8,128)}, f32[1024,1024]{1,0:T(8,128)S(1)}, u32[]{:S(2)}) copy-start(f32[1024,1024]{1,0:T(8,128)S(1)} %convert_element_type.314) | copy-start | bytes 12582916
  49.2 23.5 %copy-start.46 = (f32[1024]{0:T(1024)S(1)}, f32[1024]{0:T(1024)}, u32[]{:S(2)}) copy-start(f32[1024]{0:T(1024)} %param.22) | copy-start | bytes 12292
  49.2 24.7 %copy-start.54 = (f32[1024]{0:T(1024)S(1)}, f32[1024]{0:T(1024)}, u32[]{:S(2)}) copy-start(f32[1024]{0:T(1024)} %copy-done.52) | copy-start | bytes 12292
  74.0 13.7 %collective-permute-start.2 = (bf16[512,1024]{1,0:T(8,128)(2,1)}, bf16[512,1024]{1,0:T(8,128)(2,1)}, u32[]{:S(2)}, u32[]{:S(2)}) collective-permute-start(bf16[512,1024]{1,0:T(8,128)(2,1)} %multiply_convert_fusion.4), channel_id=1, source_target_pairs={{0,1},{1,0},{2,3},{3,2},{4,5},{5,4},{6,7},{7,6},{8,9},{9,8},{10,11... | collective-permute-start | bytes 3145736 | tf_op jit(solution)/shard_map/ppermute | solution.py:76
  74.0 13.0 %copy-start.47 = (f32[512]{0:T(512)}, f32[512]{0:T(512)S(1)}, u32[]{:S(2)}) copy-start(f32[512]{0:T(512)S(1)} %dynamic-slice.3) | copy-start | bytes 6148
  89.7 14.3 %copy-start.17 = (bf16[2,512,1024]{2,1,0:T(8,128)(2,1)}, bf16[2,512,1024]{2,1,0:T(8,128)(2,1)S(1)}, u32[]{:S(2)}) copy-start(bf16[2,512,1024]{2,1,0:T(8,128)(2,1)S(1)} %pad_maximum_fusion) | copy-start | bytes 6291460
  90.1 7.1 %copy-start.20 = (bf16[16,1024,128]{1,2,0:T(8,128)(2,1)S(1)}, bf16[16,1024,128]{1,2,0:T(8,128)(2,1)}, u32[]{:S(2)}) copy-start(bf16[16,1024,128]{1,2,0:T(8,128)(2,1)} %copy.71) | copy-start | bytes 12582916
  97.2 6.8 %copy-start.41 = (bf16[1024,16]{0,1:T(8,128)(2,1)S(1)}, bf16[1024,16]{0,1:T(8,128)(2,1)}, u32[]{:S(2)}) copy-start(bf16[1024,16]{0,1:T(8,128)(2,1)} %param.23) | copy-start | bytes 98308
  97.2 7.5 %copy-start.64 = (s32[1,1024]{1,0:T(1,128)S(1)}, s32[1,1024]{1,0:T(1,128)}, u32[]{:S(2)}) copy-start(s32[1,1024]{1,0:T(1,128)} %param.30) | copy-start | bytes 12292
  131.0 7.6 %copy-start.58 = (bf16[16,128,1024]{2,1,0:T(8,128)(2,1)S(1)}, bf16[16,128,1024]{2,1,0:T(8,128)(2,1)}, u32[]{:S(2)}) copy-start(bf16[16,128,1024]{2,1,0:T(8,128)(2,1)} %param.26) | copy-start | bytes 12582916
  131.0 7.6 %copy-start.66 = (bf16[1024,16,128]{0,2,1:T(8,128)(2,1)S(1)}, bf16[1024,16,128]{0,2,1:T(8,128)(2,1)}, u32[]{:S(2)}) copy-start(bf16[1024,16,128]{0,2,1:T(8,128)(2,1)} %get-tuple-element.28) | copy-start | bytes 12582916
  145.5 10.8 %copy-start.9 = (bf16[16,16,8,8,128]{4,3,1,0,2:T(8,128)(2,1)}, bf16[16,16,8,8,128]{4,3,1,0,2:T(8,128)(2,1)S(1)}, u32[]{:S(2)}) copy-start(bf16[16,16,8,8,128]{4,3,1,0,2:T(8,128)(2,1)S(1)} %copy.117) | copy-start | bytes 12582916
  147.1 65.6 %collective-permute-start.35 = (bf16[4,16,128,128]{3,2,1,0:T(8,128)(2,1)}, bf16[4,16,128,128]{3,2,1,0:T(8,128)(2,1)}, u32[]{:S(2)}, u32[]{:S(2)}) collective-permute-start(bf16[4,16,128,128]{3,2,1,0:T(8,128)(2,1)} %dynamic-slice_bitcast_fusion), channel_id=1, source_target_pairs={{0,4},{4,0},{8,12},{12,8},{16,20},{20,16},{24,28},{28,24},{1,5},{5... | collective-permute-start | bytes 6291464 | tf_op jit(solution)/shard_map/ppermute | solution.py:90
  180.2 60.6 %collective-permute-start.31 = (bf16[4,16,128,128]{3,2,1,0:T(8,128)(2,1)}, bf16[4,16,128,128]{3,2,1,0:T(8,128)(2,1)}, u32[]{:S(2)}, u32[]{:S(2)}) collective-permute-start(bf16[4,16,128,128]{3,2,1,0:T(8,128)(2,1)} %dynamic-slice_bitcast_fusion.1), channel_id=1, source_target_pairs={{0,4},{4,0},{8,12},{12,8},{16,20},{20,16},{24,28},{28,24},{1,5},{5... | collective-permute-start | bytes 6291464 | tf_op jit(solution)/shard_map/ppermute | solution.py:90
  193.4 18.4 %collective-permute-start.3 = (bf16[512,1024]{1,0:T(8,128)(2,1)S(1)}, bf16[512,1024]{1,0:T(8,128)(2,1)S(1)}, u32[]{:S(2)}, u32[]{:S(2)}) collective-permute-start(bf16[512,1024]{1,0:T(8,128)(2,1)S(1)} %constant_dynamic-slice_fusion.9), channel_id=1, source_target_pairs={{0,1},{1,0},{2,3},{3,2},{4,5},{5,4},{6,7},{7,6},{8,9},{9,8},{10,11... | collective-permute-start | bytes 3145736 | tf_op jit(solution)/shard_map/ppermute | solution.py:69
  193.7 11.6 %copy-start.7 = (bf16[16,8,128,128]{3,2,0,1:T(8,128)(2,1)S(1)}, bf16[16,8,128,128]{3,2,0,1:T(8,128)(2,1)}, u32[]{:S(2)}) copy-start(bf16[16,8,128,128]{3,2,0,1:T(8,128)(2,1)} %copy.85) | copy-start | bytes 12582916
  193.8 10.1 %collective-permute-start.8 = (f32[512,16]{0,1:T(8,128)S(1)}, f32[512,16]{0,1:T(8,128)S(1)}, u32[]{:S(2)}, u32[]{:S(2)}) collective-permute-start(f32[512,16]{0,1:T(8,128)S(1)} %constant_dynamic-slice_fusion.7), channel_id=1, source_target_pairs={{0,1},{1,0},{2,3},{3,2},{4,5},{5,4},{6,7},{7,6},{8,9},{9,8},{10,11... | collective-permute-start | bytes 98312 | tf_op jit(solution)/shard_map/ppermute | solution.py:69
  203.6 6.1 %collective-permute-start.6 = (bf16[512,1024]{1,0:T(8,128)(2,1)S(1)}, bf16[512,1024]{1,0:T(8,128)(2,1)S(1)}, u32[]{:S(2)}, u32[]{:S(2)}) collective-permute-start(bf16[512,1024]{1,0:T(8,128)(2,1)S(1)} %constant_dynamic-slice_fusion.8), channel_id=1, source_target_pairs={{0,1},{1,0},{2,3},{3,2},{4,5},{5,4},{6,7},{7,6},{8,9},{9,8},{10,11... | collective-permute-start | bytes 3145736 | tf_op jit(solution)/shard_map/ppermute | solution.py:69
  203.8 4.0 collective-permute-start.9
  205.6 7.0 %copy-start.10 = (bf16[16,16,8,8,128]{4,3,1,0,2:T(8,128)(2,1)S(1)}, bf16[16,16,8,8,128]{4,3,1,0,2:T(8,128)(2,1)}, u32[]{:S(2)}) copy-start(bf16[16,16,8,8,128]{4,3,1,0,2:T(8,128)(2,1)} %copy-done.9) | copy-start | bytes 12582916
  207.8 77.4 %collective-permute-start.27 = (bf16[4,16,128,128]{3,2,1,0:T(8,128)(2,1)S(1)}, bf16[4,16,128,128]{3,2,1,0:T(8,128)(2,1)S(1)}, u32[]{:S(2)}, u32[]{:S(2)}) collective-permute-start(bf16[4,16,128,128]{3,2,1,0:T(8,128)(2,1)S(1)} %dynamic-slice_bitcast_fusion.2), channel_id=1, source_target_pairs={{0,4},{4,0},{8,12},{12,8},{16,20},{20,16},{24,28},{28,24},{1,5},{5... | collective-permute-start | bytes 6291464 | tf_op jit(solution)/shard_map/ppermute | solution.py:90
  210.1 36.2 %collective-permute-start.7 = (bf16[512,1024]{1,0:T(8,128)(2,1)S(1)}, bf16[512,1024]{1,0:T(8,128)(2,1)S(1)}, u32[]{:S(2)}, u32[]{:S(2)}) collective-permute-start(bf16[512,1024]{1,0:T(8,128)(2,1)S(1)} %add_convert_fusion.1), channel_id=1, source_target_pairs={{0,2},{1,3},{2,0},{3,1},{4,6},{5,7},{6,4},{7,5},{8,10},{9,11},{10,... | collective-permute-start | bytes 3145736 | tf_op jit(solution)/shard_map/ppermute | solution.py:71
  212.2 31.4 %copy-start.8 = (bf16[16,8,128,128]{3,2,0,1:T(8,128)(2,1)S(1)}, bf16[16,8,128,128]{3,2,0,1:T(8,128)(2,1)}, u32[]{:S(2)}) copy-start(bf16[16,8,128,128]{3,2,0,1:T(8,128)(2,1)} %copy.86) | copy-start | bytes 12582916
  212.3 74.8 %collective-permute-start.4 = (bf16[512,1024]{1,0:T(8,128)(2,1)S(1)}, bf16[512,1024]{1,0:T(8,128)(2,1)S(1)}, u32[]{:S(2)}, u32[]{:S(2)}) collective-permute-start(bf16[512,1024]{1,0:T(8,128)(2,1)S(1)} %add_convert_fusion.3), channel_id=1, source_target_pairs={{0,2},{1,3},{2,0},{3,1},{4,6},{5,7},{6,4},{7,5},{8,10},{9,11},{10,... | collective-permute-start | bytes 3145736 | tf_op jit(solution)/shard_map/ppermute | solution.py:71
  216.4 74.4 %collective-permute-start.36 = (bf16[16,128,128]{2,1,0:T(8,128)(2,1)}, bf16[16,128,128]{2,1,0:T(8,128)(2,1)}, u32[]{:S(2)}, u32[]{:S(2)}) collective-permute-start(bf16[16,128,128]{2,1,0:T(8,128)(2,1)} %get-tuple-element.30), channel_id=1, source_target_pairs={{0,8},{4,12},{8,16},{12,20},{16,24},{20,28},{24,0},{28,4},{1,9},{5... | collective-permute-start | bytes 1572872 | tf_op jit(solution)/shard_map/ppermute | solution.py:95
  240.8 51.4 %collective-permute-start.37 = (bf16[16,128,128]{2,1,0:T(8,128)(2,1)}, bf16[16,128,128]{2,1,0:T(8,128)(2,1)}, u32[]{:S(2)}, u32[]{:S(2)}) collective-permute-start(bf16[16,128,128]{2,1,0:T(8,128)(2,1)} %get-tuple-element.32), channel_id=1, source_target_pairs={{0,16},{4,20},{8,24},{12,28},{16,0},{20,4},{24,8},{28,12},{1,17},{... | collective-permute-start | bytes 1572872 | tf_op jit(solution)/shard_map/ppermute | solution.py:95
  246.0 43.6 %copy-start.40 = (bf16[1024,1024]{1,0:T(8,128)(2,1)S(1)}, bf16[1024,1024]{1,0:T(8,128)(2,1)}, u32[]{:S(2)}) copy-start(bf16[1024,1024]{1,0:T(8,128)(2,1)} %param.31) | copy-start | bytes 6291460
  246.3 46.9 %collective-permute-start.38 = (bf16[16,128,128]{2,1,0:T(8,128)(2,1)S(1)}, bf16[16,128,128]{2,1,0:T(8,128)(2,1)}, u32[]{:S(2)}, u32[]{:S(2)}) collective-permute-start(bf16[16,128,128]{2,1,0:T(8,128)(2,1)S(1)} %get-tuple-element.31), channel_id=1, source_target_pairs={{0,24},{4,28},{8,0},{12,4},{16,8},{20,12},{24,16},{28,20},{1,25},{... | collective-permute-start | bytes 1572872 | tf_op jit(solution)/shard_map/ppermute | solution.py:95
  285.2 16.8 %collective-permute-start.32 = (bf16[16,128,128]{2,1,0:T(8,128)(2,1)S(1)}, bf16[16,128,128]{2,1,0:T(8,128)(2,1)}, u32[]{:S(2)}, u32[]{:S(2)}) collective-permute-start(bf16[16,128,128]{2,1,0:T(8,128)(2,1)S(1)} %get-tuple-element.33), channel_id=1, source_target_pairs={{0,8},{4,12},{8,16},{12,20},{16,24},{20,28},{24,0},{28,4},{1,9},{5... | collective-permute-start | bytes 1572872 | tf_op jit(solution)/shard_map/ppermute | solution.py:95
  287.0 38.4 %collective-permute-start.33 = (bf16[16,128,128]{2,1,0:T(8,128)(2,1)S(1)}, bf16[16,128,128]{2,1,0:T(8,128)(2,1)}, u32[]{:S(2)}, u32[]{:S(2)}) collective-permute-start(bf16[16,128,128]{2,1,0:T(8,128)(2,1)S(1)} %get-tuple-element.35), channel_id=1, source_target_pairs={{0,16},{4,20},{8,24},{12,28},{16,0},{20,4},{24,8},{28,12},{1,17},{... | collective-permute-start | bytes 1572872 | tf_op jit(solution)/shard_map/ppermute | solution.py:95
  290.8 66.5 %collective-permute-start.34 = (bf16[16,128,128]{2,1,0:T(8,128)(2,1)S(1)}, bf16[16,128,128]{2,1,0:T(8,128)(2,1)S(1)}, u32[]{:S(2)}, u32[]{:S(2)}) collective-permute-start(bf16[16,128,128]{2,1,0:T(8,128)(2,1)S(1)} %get-tuple-element.34), channel_id=1, source_target_pairs={{0,24},{4,28},{8,0},{12,4},{16,8},{20,12},{24,16},{28,20},{1,25},{... | collective-permute-start | bytes 1572872 | tf_op jit(solution)/shard_map/ppermute | solution.py:95
  292.2 79.2 %collective-permute-start.10 = (bf16[512,1024]{1,0:T(8,128)(2,1)S(1)}, bf16[512,1024]{1,0:T(8,128)(2,1)S(1)}, u32[]{:S(2)}, u32[]{:S(2)}) collective-permute-start(bf16[512,1024]{1,0:T(8,128)(2,1)S(1)} %get-tuple-element.16), channel_id=1, source_target_pairs={{0,1},{1,0},{2,3},{3,2},{4,5},{5,4},{6,7},{7,6},{8,9},{9,8},{10,11... | collective-permute-start | bytes 3145736 | tf_op jit(solution)/shard_map/ppermute | solution.py:76
  293.2 66.6 %collective-permute-start.28 = (bf16[16,128,128]{2,1,0:T(8,128)(2,1)S(1)}, bf16[16,128,128]{2,1,0:T(8,128)(2,1)S(1)}, u32[]{:S(2)}, u32[]{:S(2)}) collective-permute-start(bf16[16,128,128]{2,1,0:T(8,128)(2,1)S(1)} %get-tuple-element.36), channel_id=1, source_target_pairs={{0,8},{4,12},{8,16},{12,20},{16,24},{20,28},{24,0},{28,4},{1,9},{5... | collective-permute-start | bytes 1572872 | tf_op jit(solution)/shard_map/ppermute | solution.py:95
  302.1 66.3 %collective-permute-start.29 = (bf16[16,128,128]{2,1,0:T(8,128)(2,1)S(1)}, bf16[16,128,128]{2,1,0:T(8,128)(2,1)S(1)}, u32[]{:S(2)}, u32[]{:S(2)}) collective-permute-start(bf16[16,128,128]{2,1,0:T(8,128)(2,1)S(1)} %get-tuple-element.38), channel_id=1, source_target_pairs={{0,16},{4,20},{8,24},{12,28},{16,0},{20,4},{24,8},{28,12},{1,17},{... | collective-permute-start | bytes 1572872 | tf_op jit(solution)/shard_map/ppermute | solution.py:95
  325.5 44.6 %collective-permute-start.30 = (bf16[16,128,128]{2,1,0:T(8,128)(2,1)S(1)}, bf16[16,128,128]{2,1,0:T(8,128)(2,1)S(1)}, u32[]{:S(2)}, u32[]{:S(2)}) collective-permute-start(bf16[16,128,128]{2,1,0:T(8,128)(2,1)S(1)} %get-tuple-element.37), channel_id=1, source_target_pairs={{0,24},{4,28},{8,0},{12,4},{16,8},{20,12},{24,16},{28,20},{1,25},{... | collective-permute-start | bytes 1572872 | tf_op jit(solution)/shard_map/ppermute | solution.py:95
  357.2 39.2 %collective-permute-start.5 = (bf16[512,1024]{1,0:T(8,128)(2,1)S(1)}, bf16[512,1024]{1,0:T(8,128)(2,1)}, u32[]{:S(2)}, u32[]{:S(2)}) collective-permute-start(bf16[512,1024]{1,0:T(8,128)(2,1)S(1)} %get-tuple-element.43), channel_id=1, source_target_pairs={{0,1},{1,0},{2,3},{3,2},{4,5},{5,4},{6,7},{7,6},{8,9},{9,8},{10,11... | collective-permute-start | bytes 3145736 | tf_op jit(solution)/shard_map/ppermute | solution.py:76
  391.7 7.7 %collective-permute-start.11 = (bf16[512,1024]{1,0:T(8,128)(2,1)S(1)}, bf16[512,1024]{1,0:T(8,128)(2,1)S(1)}, u32[]{:S(2)}, u32[]{:S(2)}) collective-permute-start(bf16[512,1024]{1,0:T(8,128)(2,1)S(1)} %constant_dynamic-slice_fusion.6), channel_id=1, source_target_pairs={{0,1},{1,0},{2,3},{3,2},{4,5},{5,4},{6,7},{7,6},{8,9},{9,8},{10,11... | collective-permute-start | bytes 3145736 | tf_op jit(solution)/shard_map/ppermute | solution.py:69
  392.6 9.2 %collective-permute-start.18 = (bf16[4,256,128]{2,1,0:T(8,128)(2,1)S(1)}, bf16[4,256,128]{2,1,0:T(8,128)(2,1)S(1)}, u32[]{:S(2)}, u32[]{:S(2)}) collective-permute-start(bf16[4,256,128]{2,1,0:T(8,128)(2,1)S(1)} %dynamic-slice_bitcast_fusion.13), channel_id=1, source_target_pairs={{0,4},{4,0},{8,12},{12,8},{16,20},{20,16},{24,28},{28,24},{1,5},{5... | collective-permute-start | bytes 786440 | tf_op jit(solution)/shard_map/ppermute | solution.py:90
  395.9 18.6 %collective-permute-start.14 = (bf16[4,128,512]{2,1,0:T(8,128)(2,1)S(1)}, bf16[4,128,512]{2,1,0:T(8,128)(2,1)S(1)}, u32[]{:S(2)}, u32[]{:S(2)}) collective-permute-start(bf16[4,128,512]{2,1,0:T(8,128)(2,1)S(1)} %dynamic-slice_bitcast_fusion.12), channel_id=1, source_target_pairs={{0,4},{4,0},{8,12},{12,8},{16,20},{20,16},{24,28},{28,24},{1,5},{5... | collective-permute-start | bytes 1572872 | tf_op jit(solution)/shard_map/ppermute | solution.py:90
  399.3 33.7 %copy-start.6 = (f32[1024,1024]{1,0:T(8,128)S(1)}, f32[1024,1024]{1,0:T(8,128)}, u32[]{:S(2)}) copy-start(f32[1024,1024]{1,0:T(8,128)} %copy-done.5) | copy-start | bytes 12582916
  399.3 33.7 %copy-start.48 = (f32[512]{0:T(512)S(1)}, f32[512]{0:T(512)}, u32[]{:S(2)}) copy-start(f32[512]{0:T(512)} %copy-done.47) | copy-start | bytes 6148
  399.7 33.3 %collective-permute-start.12 = (bf16[512,1024]{1,0:T(8,128)(2,1)S(1)}, bf16[512,1024]{1,0:T(8,128)(2,1)S(1)}, u32[]{:S(2)}, u32[]{:S(2)}) collective-permute-start(bf16[512,1024]{1,0:T(8,128)(2,1)S(1)} %add_convert_fusion), channel_id=1, source_target_pairs={{0,2},{1,3},{2,0},{3,1},{4,6},{5,7},{6,4},{7,5},{8,10},{9,11},{10,... | collective-permute-start | bytes 3145736 | tf_op jit(solution)/shard_map/ppermute | solution.py:71
  402.0 20.9 %collective-permute-start.19 = (bf16[256,128]{1,0:T(8,128)(2,1)S(1)}, bf16[256,128]{1,0:T(8,128)(2,1)S(1)}, u32[]{:S(2)}, u32[]{:S(2)}) collective-permute-start(bf16[256,128]{1,0:T(8,128)(2,1)S(1)} %get-tuple-element.63), channel_id=1, source_target_pairs={{0,8},{4,12},{8,16},{12,20},{16,24},{20,28},{24,0},{28,4},{1,9},{5... | collective-permute-start | bytes 196616 | tf_op jit(solution)/shard_map/ppermute | solution.py:95
  412.0 12.4 %collective-permute-start.20 = (bf16[256,128]{1,0:T(8,128)(2,1)S(1)}, bf16[256,128]{1,0:T(8,128)(2,1)S(1)}, u32[]{:S(2)}, u32[]{:S(2)}) collective-permute-start(bf16[256,128]{1,0:T(8,128)(2,1)S(1)} %get-tuple-element.65), channel_id=1, source_target_pairs={{0,16},{4,20},{8,24},{12,28},{16,0},{20,4},{24,8},{28,12},{1,17},{... | collective-permute-start | bytes 196616 | tf_op jit(solution)/shard_map/ppermute | solution.py:95
  413.6 23.3 %copy-start.56 = (f32[512,1]{0,1:T(1,128)S(1)}, f32[512,1]{0,1:T(1,128)}, u32[]{:S(2)}) copy-start(f32[512,1]{0,1:T(1,128)} %multiply_multiply_fusion) | copy-start | bytes 6148
  413.6 11.9 %collective-permute-start.21 = (bf16[256,128]{1,0:T(8,128)(2,1)S(1)}, bf16[256,128]{1,0:T(8,128)(2,1)S(1)}, u32[]{:S(2)}, u32[]{:S(2)}) collective-permute-start(bf16[256,128]{1,0:T(8,128)(2,1)S(1)} %get-tuple-element.64), channel_id=1, source_target_pairs={{0,24},{4,28},{8,0},{12,4},{16,8},{20,12},{24,16},{28,20},{1,25},{... | collective-permute-start | bytes 196616 | tf_op jit(solution)/shard_map/ppermute | solution.py:95
  414.7 13.7 %collective-permute-start.15 = (bf16[128,512]{1,0:T(8,128)(2,1)S(1)}, bf16[128,512]{1,0:T(8,128)(2,1)S(1)}, u32[]{:S(2)}, u32[]{:S(2)}) collective-permute-start(bf16[128,512]{1,0:T(8,128)(2,1)S(1)} %get-tuple-element.56), channel_id=1, source_target_pairs={{0,8},{4,12},{8,16},{12,20},{16,24},{20,28},{24,0},{28,4},{1,9},{5... | collective-permute-start | bytes 393224 | tf_op jit(solution)/shard_map/ppermute | solution.py:95
  422.9 10.1 %collective-permute-start.16 = (bf16[128,512]{1,0:T(8,128)(2,1)S(1)}, bf16[128,512]{1,0:T(8,128)(2,1)S(1)}, u32[]{:S(2)}, u32[]{:S(2)}) collective-permute-start(bf16[128,512]{1,0:T(8,128)(2,1)S(1)} %get-tuple-element.58), channel_id=1, source_target_pairs={{0,16},{4,20},{8,24},{12,28},{16,0},{20,4},{24,8},{28,12},{1,17},{... | collective-permute-start | bytes 393224 | tf_op jit(solution)/shard_map/ppermute | solution.py:95
  424.5 8.5 %collective-permute-start.17 = (bf16[128,512]{1,0:T(8,128)(2,1)S(1)}, bf16[128,512]{1,0:T(8,128)(2,1)S(1)}, u32[]{:S(2)}, u32[]{:S(2)}) collective-permute-start(bf16[128,512]{1,0:T(8,128)(2,1)S(1)} %get-tuple-element.57), channel_id=1, source_target_pairs={{0,24},{4,28},{8,0},{12,4},{16,8},{20,12},{24,16},{28,20},{1,25},{... | collective-permute-start | bytes 393224 | tf_op jit(solution)/shard_map/ppermute | solution.py:95
  433.8 1.4 collective-permute-start.22
  435.3 4.2 collective-permute-start.23
  437.6 11.3 %collective-permute-start.13 = (bf16[512,1024]{1,0:T(8,128)(2,1)S(1)}, bf16[512,1024]{1,0:T(8,128)(2,1)S(1)}, u32[]{:S(2)}, u32[]{:S(2)}) collective-permute-start(bf16[512,1024]{1,0:T(8,128)(2,1)S(1)} %subtract_convert_fusion), channel_id=1, source_target_pairs={{0,1},{1,0},{2,3},{3,2},{4,5},{5,4},{6,7},{7,6},{8,9},{9,8},{10,11... | collective-permute-start | bytes 3145736 | tf_op jit(solution)/shard_map/ppermute | solution.py:76
  439.5 7.1 %collective-permute-start.24 = (f32[18,128]{1,0:T(8,128)S(1)}, f32[18,128]{1,0:T(8,128)S(1)}, u32[]{:S(2)}, u32[]{:S(2)}) collective-permute-start(f32[18,128]{1,0:T(8,128)S(1)} %get-tuple-element.70), channel_id=1, source_target_pairs={{0,8},{4,12},{8,16},{12,20},{16,24},{20,28},{24,0},{28,4},{1,9},{5... | collective-permute-start | bytes 27656 | tf_op jit(solution)/shard_map/ppermute | solution.py:95
  442.9 4.6 %collective-permute-start.25 = (f32[18,128]{1,0:T(8,128)S(1)}, f32[18,128]{1,0:T(8,128)S(1)}, u32[]{:S(2)}, u32[]{:S(2)}) collective-permute-start(f32[18,128]{1,0:T(8,128)S(1)} %get-tuple-element.72), channel_id=1, source_target_pairs={{0,16},{4,20},{8,24},{12,28},{16,0},{20,4},{24,8},{28,12},{1,17},{... | collective-permute-start | bytes 27656 | tf_op jit(solution)/shard_map/ppermute | solution.py:95
  444.2 3.7 collective-permute-start.26
  (46 other events, 151.4 us)

commit v2 on v1

--- a/solution.py
+++ b/solution.py
@@ -1,6 +1,10 @@
+import functools
+
 import jax
 import jax.numpy as jnp
 from jax import lax
+from jax.experimental import pallas as pl
+from jax.experimental.pallas import tpu as pltpu
 from jax.sharding import PartitionSpec as P
 
 MODEL_WIDTH = 1024
@@ -65,9 +69,9 @@
 def reduce_half(part, core):
     half = part.shape[0] // 2
     mine = lax.dynamic_slice_in_dim(part, core * half, half, 0)
-    other = lax.dynamic_slice_in_dim(part, (1 - core) * half, half, 0)
+    other = lax.dynamic_slice_in_dim(part, (1 - core) * half, half, 0).astype(BF16)
     got = lax.ppermute(other, "tensor", CORE_PAIRS)
-    total = (mine.astype(F32) + got.astype(F32)).astype(part.dtype)
+    total = (mine + got.astype(F32)).astype(BF16)
     far = lax.ppermute(total, "tensor", X_PAIRS)
     return total.astype(F32) + far.astype(F32)
 
@@ -78,25 +82,222 @@
     return pair.reshape((2 * half_rows.shape[0],) + half_rows.shape[1:])
 
 
-def scatter_sum(blocks, ways):
+def bits_of(ways):
+    return tuple(range(ways.bit_length() - 1))
+
+
+def flip(array, ways, bit):
+    return lax.ppermute(array, "dp", [(i, i ^ (1 << bit)) for i in range(ways)])
+
+
+def halve(keep, send, ways, order):
+    got = flip(send, ways, order[0])
+    for bit in order[1:]:
+        half = keep.shape[0] // 2
+        to_send = (keep[half:].astype(F32) + got[half:].astype(F32)).astype(keep.dtype)
+        keep = (keep[:half].astype(F32) + got[:half].astype(F32)).astype(keep.dtype)
+        got = flip(to_send, ways, bit)
+    return (keep.astype(F32) + got.astype(F32))[0]
+
+
+def scatter_sum(blocks, ways, order):
     me = lax.axis_index("dp")
-    if ways != 8:
-        return lax.psum_scatter(blocks, "dp", scatter_dimension=0, tiled=False).astype(F32)
-    y = me % 2
-    z = me // 2
-    grid = blocks.reshape((4, 2) + blocks.shape[1:])
-    mine = lax.dynamic_index_in_dim(grid, y, 1, keepdims=False)
-    other = lax.dynamic_index_in_dim(grid, 1 - y, 1, keepdims=False)
-    got = lax.ppermute(other, "dp", [(i, i ^ 1) for i in range(8)])
-    summed = (mine.astype(F32) + got.astype(F32)).astype(blocks.dtype)
-    total = lax.dynamic_index_in_dim(summed, z, 0, keepdims=False).astype(F32)
-    for step in (1, 2, 3):
-        block = lax.dynamic_index_in_dim(summed, (z + step) % 4, 0, keepdims=False)
-        arrived = lax.ppermute(
-            block, "dp", [(i, (i + 2 * step) % 8) for i in range(8)]
-        )
-        total = total + arrived.astype(F32)
-    return total
+    count = len(order)
+    current = blocks.reshape((2,) * count + blocks.shape[1:])
+    left = list(reversed(range(count)))
+    for bit in order:
+        axis = left.index(bit)
+        mine_at = (me >> bit) & 1
+        mine = lax.dynamic_index_in_dim(current, mine_at, axis, keepdims=False)
+        other = lax.dynamic_index_in_dim(current, 1 - mine_at, axis, keepdims=False)
+        got = flip(other, ways, bit)
+        total = mine.astype(F32) + got.astype(F32)
+        left.remove(bit)
+        current = total.astype(blocks.dtype) if left else total
+    return current
+
+
+QUAD = 4
+ROWS = 256
+
+
+def expert_kernel(first, quads, ways, orders, carried, *refs):
+    x_ref, xt_ref, dy_ref, dyt_ref, gate_ref, wg_ref, wu_ref, wd_ref = refs[:8]
+    refs = refs[8:]
+    if carried:
+        norm_in, moe_in = refs[:2]
+        refs = refs[2:]
+    dg_ref, norm_out, moe_out = refs[:3]
+    keeps = refs[3 : 3 + quads]
+    sends = refs[3 + quads : 3 + 2 * quads]
+    wgu, gu, gated, grads, norm_acc, moe_acc, block_sem, acc_sem = refs[3 + 2 * quads :]
+    step = pl.program_id(0)
+    rows, width = x_ref.shape
+    ff = wg_ref.shape[2]
+    piece = width // ways
+    me = lax.axis_index("dp")
+    load_norm = load_moe = None
+    if carried:
+        load_norm = pltpu.make_async_copy(norm_in, norm_acc, acc_sem.at[0])
+        load_moe = pltpu.make_async_copy(moe_in, moe_acc, acc_sem.at[1])
+
+        @pl.when(step == 0)
+        def _():
+            load_norm.start()
+            load_moe.start()
+
+    @pl.when(step == 0)
+    def _():
+        dg_ref[...] = jnp.zeros_like(dg_ref)
+
+    for j in range(QUAD):
+        wgu[:, 2 * j * ff : (2 * j + 1) * ff] = wg_ref[j]
+        wgu[:, (2 * j + 1) * ff : (2 * j + 2) * ff] = wu_ref[j]
+    lane = lax.broadcasted_iota(jnp.int32, (ROWS, dg_ref.shape[1]), 1)
+
+    def hidden_rows(i, _):
+        at = pl.ds(pl.multiple_of(i * ROWS, ROWS), ROWS)
+        au = mm(x_ref[at, :], wgu[...], ((1,), (0,)))
+        down = mm(dy_ref[at, :], wd_ref[...].reshape(QUAD * ff, width), ((1,), (1,)))
+        gate_rows = gate_ref[0, at, :]
+        dg = dg_ref[at, :]
+        for j in range(QUAD):
+            pre = au[:, 2 * j * ff : (2 * j + 1) * ff]
+            up = au[:, (2 * j + 1) * ff : (2 * j + 2) * ff]
+            back = down[:, j * ff : (j + 1) * ff]
+            gate = gate_rows[:, j : j + 1]
+            sigmoid = 1.0 / (1.0 + jnp.exp(-pre))
+            act = pre * sigmoid
+            hidden = act * up
+            gated[at, j * ff : (j + 1) * ff] = (gate * hidden).astype(BF16)
+            row = jnp.sum(hidden * back, axis=1, keepdims=True)
+            dg = jnp.where(lane == (first + step) * QUAD + j, row, dg)
+            back = gate * back
+            slope = sigmoid * (1.0 + pre * (1.0 - sigmoid))
+            gu[at, 2 * j * ff : (2 * j + 1) * ff] = (back * up * slope).astype(BF16)
+            gu[at, (2 * j + 1) * ff : (2 * j + 2) * ff] = (back * act).astype(BF16)
+        dg_ref[at, :] = dg
+        return 0
+
+    lax.fori_loop(0, rows // ROWS, hidden_rows, 0)
+
+    def copies(chunk):
+        out = []
+        for slot in range(ways):
+            dest = 0
+            for place, bit in enumerate(orders[chunk]):
+                own = (slot >> (len(orders[chunk]) - 1 - place)) & 1
+                dest = dest + ((me // (1 << bit) + own) % 2) * (1 << bit)
+            block = grads.at[pl.ds(pl.multiple_of(dest * piece, piece), piece), :]
+            half = ways // 2
+            target = keeps[chunk].at[slot] if slot < half else sends[chunk].at[slot - half]
+            out.append(pltpu.make_async_copy(block, target, block_sem.at[slot]))
+        return out
+
+    if quads > 1:
+
+        @pl.when(step > 0)
+        def _():
+            for copy in copies(0):
+                copy.wait()
+
+    def grad_rows(i, _):
+        at = pl.ds(pl.multiple_of(i * ROWS, ROWS), ROWS)
+        grads[at, : 2 * QUAD * ff] = mm(xt_ref[at, :], gu[...], ((1,), (0,))).astype(BF16)
+        grads[at, 2 * QUAD * ff :] = mm(dyt_ref[at, :], gated[...], ((1,), (0,))).astype(BF16)
+        return 0
+
+    lax.fori_loop(0, width // ROWS, grad_rows, 0)
+    for chunk in range(quads):
+
+        @pl.when(step == chunk)
+        def _():
+            for copy in copies(chunk):
+                copy.start()
+
+    if carried:
+
+        @pl.when(step == 0)
+        def _():
+            load_norm.wait()
+            load_moe.wait()
+
+    def data_rows(i, _):
+        at = pl.ds(pl.multiple_of(i * ROWS, ROWS), ROWS)
+        norm = mm(gu[at, :], wgu[...], ((1,), (1,)))
+        moe = mm(gated[at, :], wd_ref[...].reshape(QUAD * ff, width), ((1,), (0,)))
+        if carried:
+            norm_acc[at, :] += norm
+            moe_acc[at, :] += moe
+        else:
+            norm_acc[at, :] = norm
+            moe_acc[at, :] = moe
+        return 0
+
+    lax.fori_loop(0, rows // ROWS, data_rows, 0)
+
+    @pl.when(step == quads - 1)
+    def _():
+        save_norm = pltpu.make_async_copy(norm_acc, norm_out, acc_sem.at[0])
+        save_moe = pltpu.make_async_copy(moe_acc, moe_out, acc_sem.at[1])
+        save_norm.start()
+        save_moe.start()
+        for copy in copies(0):
+            copy.wait()
+        save_norm.wait()
+        save_moe.wait()
+
+
+def run_experts(first, orders, ways, x, xt, dy, dyt, gates, w_gate, w_up, w_down, carry):
+    quads = len(orders)
+    assert carry is not None or quads == 1
+    rows, width = x.shape
+    ff = w_gate.shape[2]
+    piece = width // ways
+    whole = pl.BlockSpec((rows, width), lambda s: (0, 0), pipeline_mode=pl.Buffered(1))
+    flat = pl.BlockSpec((width, rows), lambda s: (0, 0), pipeline_mode=pl.Buffered(1))
+    any_space = pl.BlockSpec(memory_space=pl.ANY)
+    wide = 3 * QUAD * ff
+    block = jax.ShapeDtypeStruct((ways // 2, piece, wide), BF16)
+    total = jax.ShapeDtypeStruct((rows, width), F32)
+    flops = 2 * 9 * quads * QUAD * rows * width * ff
+    moved = quads * QUAD * width * ff * 12 + rows * width * 8 + rows * width * 16
+    out = pl.pallas_call(
+        functools.partial(expert_kernel, first, quads, ways, orders, carry is not None),
+        grid=(quads,),
+        out_shape=(jax.ShapeDtypeStruct((rows, 128), F32), total, total) + (block,) * (2 * quads),
+        in_specs=[
+            whole,
+            flat,
+            whole,
+            flat,
+            pl.BlockSpec((1, rows, QUAD), lambda s: (first + s, 0, 0)),
+            pl.BlockSpec((QUAD, width, ff), lambda s: (first + s, 0, 0)),
+            pl.BlockSpec((QUAD, width, ff), lambda s: (first + s, 0, 0)),
+            pl.BlockSpec((QUAD, ff, width), lambda s: (first + s, 0, 0)),
+        ]
+        + ([any_space] * 2 if carry is not None else []),
+        out_specs=(pl.BlockSpec((rows, 128), lambda s: (0, 0)), any_space, any_space)
+        + (any_space,) * (2 * quads),
+        scratch_shapes=[
+            pltpu.VMEM((width, 2 * QUAD * ff), BF16),
+            pltpu.VMEM((rows, 2 * QUAD * ff), BF16),
+            pltpu.VMEM((rows, QUAD * ff), BF16),
+            pltpu.VMEM((width, wide), BF16),
+            pltpu.VMEM((rows, width), F32),
+            pltpu.VMEM((rows, width), F32),
+            pltpu.SemaphoreType.DMA((ways,)),
+            pltpu.SemaphoreType.DMA((2,)),
+        ],
+        compiler_params=pltpu.CompilerParams(
+            dimension_semantics=("arbitrary",), vmem_limit_bytes=44 << 20
+        ),
+        cost_estimate=pl.CostEstimate(
+            flops=flops, bytes_accessed=moved, transcendentals=quads * QUAD * rows * ff
+        ),
+        name="experts_" + str(first),
+    )(x, xt, dy, dyt, gates, w_gate, w_up, w_down, *(carry if carry is not None else ()))
+    return out[0], out[1], out[2], out[3 : 3 + quads], out[3 + quads :]
 
 
 def make_body(ways):
@@ -131,6 +332,10 @@
         def my_half(array):
             return lax.dynamic_slice_in_dim(array, core * half, half, 0)
 
+        from_x = lax.ppermute(w_output, "tensor", X_PAIRS)
+        near = jnp.stack([w_output, from_x])
+        far = lax.ppermute(near, "tensor", CORE_PAIRS)
+        all_output = jnp.concatenate([w_output, far[0], from_x, far[1]], axis=0)
         resid_in = tokens.astype(F32)
         inv_one = lax.rsqrt(jnp.mean(resid_in * resid_in, axis=1, keepdims=True) + epsilon)
         first_normed = (resid_in * inv_one * gain_attn).astype(BF16)
@@ -172,8 +377,11 @@
             outs.append(res.astype(BF16))
             totals.append(total)
         head_out = jnp.concatenate(outs, axis=0).reshape(rows, q_local * HEAD_SIZE)
-        attn_part = mm(head_out, w_output, ((1,), (0,))).astype(BF16)
-        mid = my_half(resid_in) + reduce_half(attn_part, core)
+        mine = my_half(head_out)
+        other = lax.dynamic_slice_in_dim(head_out, (1 - core) * half, half, 0)
+        chip_heads = jnp.concatenate([mine, lax.ppermute(other, "tensor", CORE_PAIRS)], axis=1)
+        all_heads = jnp.concatenate([chip_heads, lax.ppermute(chip_heads, "tensor", X_PAIRS)], axis=1)
+        mid = my_half(resid_in) + mm(all_heads, all_output, ((1,), (0,)))
         inv_two = lax.rsqrt(jnp.mean(mid * mid, axis=1, keepdims=True) + epsilon)
         normed_half = (mid * inv_two * gain_ffn).astype(BF16)
         normed = share_half(normed_half, core)
@@ -190,43 +398,29 @@
         gates = jnp.where(picked, gates, 0.0)
         slot_gate = gates * kept
 
-        gate_pre = jnp.einsum("td,edf->tef", normed, w_gate, preferred_element_type=F32)
-        up_pre = jnp.einsum("td,edf->tef", normed, w_up, preferred_element_type=F32)
-        dy_down = jnp.einsum("td,efd->tef", cotangent, w_down, preferred_element_type=F32)
-        sigmoid = jax.nn.sigmoid(gate_pre)
-        act = gate_pre * sigmoid
-        hidden = act * up_pre
-        gated = (slot_gate[:, :, None] * hidden).astype(BF16)
-        grad_gate_part = jnp.sum(hidden * dy_down, axis=2) * kept
-        grad_hidden = slot_gate[:, :, None] * dy_down
-        slope = sigmoid * (1.0 + gate_pre * (1.0 - sigmoid))
-        grad_a = (grad_hidden * up_pre * slope).astype(BF16)
-        grad_u = (grad_hidden * act).astype(BF16)
-        moe_part = jnp.einsum("tef,efd->td", gated, w_down, preferred_element_type=F32)
-        norm_part = jnp.einsum("tef,edf->td", grad_a, w_gate, preferred_element_type=F32)
-        norm_part = norm_part + jnp.einsum("tef,edf->td", grad_u, w_up, preferred_element_type=F32)
         piece = width // ways
-        grad_gate = jnp.einsum("td,tef->edf", normed, grad_a, preferred_element_type=F32)
-        grad_up = jnp.einsum("td,tef->edf", normed, grad_u, preferred_element_type=F32)
-        grad_down = jnp.einsum("tef,td->efd", gated, cotangent, preferred_element_type=F32)
-
-        def send_rows(grad):
-            e, d, f = grad.shape
-            return grad.astype(BF16).reshape(e, ways, d // ways, f).transpose(1, 0, 2, 3)
-
-        def send_columns(grad):
-            e, f, d = grad.shape
-            return grad.astype(BF16).reshape(e, f, ways, d // ways).transpose(2, 0, 1, 3)
-
-        sent_gate = scatter_sum(send_rows(grad_gate), ways)
-        sent_up = scatter_sum(send_rows(grad_up), ways)
-        sent_down = scatter_sum(send_columns(grad_down), ways)
-
-        norm_half = reduce_half(norm_part.astype(BF16), core)
+        ff = w_gate.shape[2]
+        plain = bits_of(ways)
+        turned = plain[1:] + plain[:1]
+        by_quad = slot_gate.reshape(rows, E // QUAD, QUAD).transpose(1, 0, 2)
+        shared = (normed, normed.T, cotangent, cotangent.T, by_quad, w_gate, w_up, w_down)
+        dg_one, norm_part, moe_part, keeps, sends = run_experts(0, (plain,), ways, *shared, None)
+        orders = (plain, turned, plain, plain)
+        dg_two, norm_part, moe_part, more_keeps, more_sends = run_experts(
+            1, orders[1:], ways, *shared, (norm_part, moe_part)
+        )
+        keeps, sends = tuple(keeps) + tuple(more_keeps), tuple(sends) + tuple(more_sends)
+        parts = [halve(keeps[c], sends[c], ways, orders[c]) for c in range(E // QUAD)]
+        quads = jnp.stack(parts)
+        gate_up = quads[:, :, : 2 * QUAD * ff].reshape(E // QUAD, piece, QUAD, 2, ff)
+        gate_up = gate_up.transpose(3, 0, 2, 1, 4).reshape(2, E, piece, ff)
+        sent_down = quads[:, :, 2 * QUAD * ff :].reshape(E // QUAD, piece, QUAD, ff)
+        sent_down = sent_down.transpose(0, 2, 3, 1).reshape(E, ff, piece)
+        grad_gate_part = (dg_one[:, :E] + dg_two[:, :E]) * kept
+
+        norm_half = reduce_half(norm_part, core)
         dg_half = reduce_half(grad_gate_part, core)
-        output = share_half(
-            (mid + reduce_half(moe_part.astype(BF16), core)).astype(BF16), core
-        )
+        output = share_half((mid + reduce_half(moe_part, core)).astype(BF16), core)
         gates_half = my_half(gates)
         dz = gates_half * (dg_half - jnp.sum(gates_half * dg_half, axis=1, keepdims=True))
         dlg = dz.astype(BF16)
@@ -240,11 +434,7 @@
             - mid * inv_two**3 * jnp.mean(scaled * mid, axis=1, keepdims=True)
         )
         grad_attn = share_half(grad_mid.astype(BF16), core)
-        grad_output = mm(head_out, grad_attn, ((0,), (0,)))
-        sent_output = scatter_sum(
-            grad_output.astype(BF16).reshape(q_local * HEAD_SIZE, ways, piece).transpose(1, 0, 2),
-            ways,
-        )
+        grad_output = mm(grad_attn, head_out, ((0,), (0,)))
         grad_heads = mm(grad_attn, w_output, ((1,), (1,))).astype(BF16)
         grad_heads = grad_heads.reshape(rows, kv_local, group, HEAD_SIZE)
         query_parts = []
@@ -273,14 +463,15 @@
         dvb = grad_v.astype(BF16).reshape(rows, -1)
         grad_qkv = jnp.concatenate([dqp, dkp, dvb], axis=1)
         w_qkv = jnp.concatenate([w_query, key_weight, value_weight], axis=1)
-        grad_wide = mm(first_normed, grad_qkv, ((0,), (0,))).astype(BF16)
-        sent_qkv = scatter_sum(grad_wide.reshape(ways, piece, -1), ways)
+        grad_wide = mm(first_normed, grad_qkv, ((0,), (0,)))
+        attn_grads = jnp.concatenate([grad_wide, grad_output], axis=1).astype(BF16)
+        sent_attn = scatter_sum(attn_grads.reshape(ways, piece, -1), ways, plain)
         nq, nk = w_query.shape[1], key_weight.shape[1]
         normed_one_part = mm(grad_qkv, w_qkv, ((1,), (1,)))
-        norm_one_half = reduce_half(normed_one_part.astype(BF16), core)
+        grad_gain_attn = jnp.sum(normed_one_part * resid_in * inv_one, axis=0)
+        norm_one_half = reduce_half(normed_one_part, core)
         x_half = my_half(resid_in)
         inv_half = my_half(inv_one)
-        grad_gain_attn = jnp.sum(norm_one_half * x_half * inv_half, axis=0)
         scaled_one = gain_attn * norm_one_half
         input_half = (
             grad_mid
@@ -288,22 +479,25 @@
             - x_half * inv_half**3 * jnp.mean(scaled_one * x_half, axis=1, keepdims=True)
         ).astype(BF16)
         input_grad = share_half(input_half, core)
-        small = jnp.concatenate([grad_gain_attn[None], grad_gain_ffn[None], grad_router], axis=0)
+        first_chip = (lax.axis_index("tensor") < 2).astype(F32)
+        row_sums = jnp.concatenate([grad_gain_ffn[None], grad_router], axis=0) * first_chip
+        small = jnp.concatenate([grad_gain_attn[None], row_sums], axis=0)
         small = small + lax.ppermute(small, "tensor", CORE_PAIRS)
+        small = small + lax.ppermute(small, "tensor", X_PAIRS)
         count = small.shape[0]
-        small = scatter_sum(small.reshape(count, ways, piece).transpose(1, 0, 2), ways)
+        small = scatter_sum(small.reshape(count, ways, piece).transpose(1, 0, 2), ways, plain)
         return (
             output,
             input_grad,
-            sent_qkv[:, :nq],
-            sent_qkv[:, nq : nq + nk],
-            sent_qkv[:, nq + nk :],
-            sent_output,
+            sent_attn[:, :nq],
+            sent_attn[:, nq : nq + nk],
+            sent_attn[:, nq + nk : nq + 2 * nk],
+            sent_attn[:, nq + 2 * nk :].T,
             small[0],
             small[1],
             small[2:].T,
-            sent_gate,
-            sent_up,
+            gate_up[0],
+            gate_up[1],
             sent_down,
         )
 

time: 457 us -> 439 us (0.961)
  starting transfers between devices: 112 us -> 32.5 us
  Pallas kernels: 0 us -> 75.5 us
  matrix products: 116 us -> 41.1 us
  waiting for transfers between devices: 117 us -> 169 us
  local copies, waits for them, and re-layouts: 57.9 us -> 65.5 us
    pallas_call x0 -> x2, Pallas kernels: none -> 75.5 us  [run_experts(): pl.pallas_call(functools.partial(expert_kernel, first, quads, ways, order...]
    ppermute x24 -> x23, starting transfers between devices: 102 us -> 27.3 us  [the longest x18 22.8 us: flip(): return lax.ppermute(array, 'dp', [(i, i ^ 1 << bit) for i in range(ways)])]
    ppermute x24 -> x23, waiting for transfers between devices: 88.1 us -> 155 us  [the longest x18 138 us: flip(): return lax.ppermute(array, 'dp', [(i, i ^ 1 << bit) for i in range(ways)])]
    dot_general x7 -> x0, matrix products: 65 us -> none  [the longest x1 25.4 us: body(): jnp.einsum('td,efd->tef', cotangent, w_down, preferred_element_type=F32)]
    unnamed x2 -> x0, matrix products: 13.9 us -> none
    ppermute x5 -> x4, waiting for transfers between devices: 25.2 us -> 14.1 us  [reduce_half(): far = lax.ppermute(total, 'tensor', X_PAIRS)]
    convert_element_type x0 -> x4, local copies, waits for them, and re-layouts: none -> 8.52 us  [reduce_half(): lax.dynamic_slice_in_dim(part, (1 - core) * half, half, 0).astype(BF16)]
    dot_general x12, matrix products: 15.5 us -> 22.3 us  [mm(): lax.dot_general(left, right, (dims, ((), ())), preferred_element_type=F32)]
  transfers between devices with their start and end apart: 39 -> 36, of which waited for: 15 -> 17; matrix products, arithmetic and copies ran while one was open for 25% -> 28% of each run, Pallas kernels for 0% -> 13%
where the time goes in v2:
time: 439 us; the launch traced here: 435 us
  waiting for transfers between devices  169 us (38%)
  Pallas kernels  75.5 us (17%)
  local copies, waits for them, and re-layouts  65.5 us (15%)
  other arithmetic  48.6 us (11%)
  matrix products  41.1 us (9%)
  starting transfers between devices  32.5 us (7%)
    ppermute x18, waiting for transfers between devices, flip(): return lax.ppermute(array, 'dp', [(i, i ^ 1 << bit) for i in range(ways)])  138 us
    pallas_call x2, Pallas kernels, run_experts(): pl.pallas_call(functools.partial(expert_kernel, first, quads, ways, order...  75.5 us
    ppermute x18, starting transfers between devices, flip(): return lax.ppermute(array, 'dp', [(i, i ^ 1 << bit) for i in range(ways)])  22.8 us
    dot_general x12, matrix products, mm(): lax.dot_general(left, right, (dims, ((), ())), preferred_element_type=F32)  22.3 us
    unnamed x162, local copies, waits for them, and re-layouts  21.7 us
    ppermute x4, waiting for transfers between devices, reduce_half(): far = lax.ppermute(total, 'tensor', X_PAIRS)  14.1 us
    ppermute x1, waiting for transfers between devices, body(): lax.ppermute(chip_heads, 'tensor', X_PAIRS)  13.5 us
    another operation x8, other arithmetic, share_half(): jnp.stack([jnp.where(core == 0, half_rows, got), jnp.where(core == 0, got...  9.46 us
  transfers between devices with their start and end apart: 36, of which 17 were waited for; matrix products, arithmetic and copies ran while one was open for 28% of the time, Pallas kernels for 13%

profile of v2, /device:TPU:0, one launch (start us, length us, event | category | flops | bytes accessed | tf_op | source)
XLA Modules:
  0.0 434.9 jit_solution(6928156858757409307)
XLA Ops:
  0.7 3.0 collective-permute-start.2
  3.7 2.1 multiply_reduce_fusion.1
  7.1 2.0 fusion.86
  15.3 1.6 fusion.4
  17.0 1.8 exponential_reduce_fusion
  20.3 1.6 convolution_convert_fusion.5
  27.8 1.6 copy-done.16
  29.4 2.9 fusion.36
  32.4 2.1 pad_maximum_fusion.6
  34.5 1.9 fusion.39
  40.1 13.5 %collective-permute-done.1 = bf16[512,512]{0,1:T(8,128)(2,1)S(1)} collective-permute-done((bf16[512,512]{0,1:T(8,128)(2,1)S(1)}, bf16[512,512]{0,1:T(8,128)(2,1)S(1)}, u32[]{:S(2)}, u32[]{:S(2)}) %collective-permute-start.1) | collective-permute-done | bytes 524320 | tf_op jit(solution)/shard_map/ppermute | solution.py:383
  53.6 2.4 multiply_reduce_fusion.5
  58.7 3.0 copy.116
  61.7 2.4 select_bitcast_fusion.7
  64.3 2.6 copy.165
  68.1 1.9 broadcast_select_fusion
  70.2 1.9 copy.123
  72.2 1.6 copy-done.4
  73.8 1.6 copy-done.6
  75.4 20.2 %experts_0.1 = (f32[1024,128]{1,0:T(8,128)S(1)}, f32[1024,1024]{1,0:T(8,128)}, f32[1024,1024]{1,0:T(8,128)}, bf16[4,128,1536]{2,1,0:T(8,128)(2,1)S(1)}, bf16[4,128,1536]{2,1,0:T(8,128)(2,1)}) custom-call(bf16[1024,1024]{1,0:T(8,128)(2,1)S(1)} %bitcast.257, bf16[1024,1024]{1,0:T(8,128)(2,1)S(1)} %bitcast.260, bf16[1024,1024]{1,0:T(8,128)(2,1)S(1)} %copy-done.4, ...), custom_call_target="tpu_custom_call" | custom-call | flops 9663676416 | bytes 31457280 | tf_op jit(solution)/shard_map/experts_0/pallas_call | solution.py:265
  98.2 55.3 %experts_1.1 = (f32[1024,128]{1,0:T(8,128)S(1)}, f32[1024,1024]{1,0:T(8,128)}, f32[1024,1024]{1,0:T(8,128)}, bf16[4,128,1536]{2,1,0:T(8,128)(2,1)S(1)}, bf16[4,1...) custom-call(bf16[1024,1024]{1,0:T(8,128)(2,1)} %bitcast.258, ...), custom_call_target="tpu_custom_call" | custom-call | flops 28991029248 | bytes 44040192 | tf_op jit(solution)/shard_map/experts_1/pallas_call | solution.py:265
  155.1 4.0 dynamic-slice_convert_fusion.1
  159.3 2.7 dynamic-slice_convert_fusion.2
  165.8 3.2 collective-permute-done.11
  173.5 1.6 collective-permute-start.33
  175.1 2.3 add_convert_fusion.1
  178.0 1.6 add_convert_fusion.3
  181.2 1.9 add_convert_fusion.11
  183.0 17.6 %collective-permute-done.27 = bf16[4,128,1536]{2,1,0:T(8,128)(2,1)S(1)} collective-permute-done((bf16[4,128,1536]{2,1,0:T(8,128)(2,1)}, bf16[4,128,1536]{2,1,0:T(8,128)(2,1)S(1)}, u32[]{:S(2)}, u32[]{:S(2)}) %collective-permute-start.27) | collective-permute-done | bytes 1572896 | tf_op jit(solution)/shard_map/ppermute | solution.py:90
  202.6 3.9 collective-permute-done.30
  206.5 2.6 collective-permute-start.28
  209.5 29.1 %collective-permute-done.33 = bf16[4,128,1536]{2,1,0:T(8,128)(2,1)S(1)} collective-permute-done((bf16[4,128,1536]{2,1,0:T(8,128)(2,1)S(1)}, bf16[4,128,1536]{2,1,0:T(8,128)(2,1)S(1)}, u32[]{:S(2)}, u32[]{:S(2)}) %collective-permute-start.33) | collective-permute-done | bytes 1572896 | tf_op jit(solution)/shard_map/ppermute | solution.py:90
  242.7 2.4 fusion.88
  245.8 2.7 collective-permute-start.26
  248.6 18.8 %collective-permute-done.31 = bf16[2,128,1536]{2,1,0:T(8,128)(2,1)S(1)} collective-permute-done((bf16[2,128,1536]{2,1,0:T(8,128)(2,1)S(1)}, bf16[2,128,1536]{2,1,0:T(8,128)(2,1)S(1)}, u32[]{:S(2)}, u32[]{:S(2)}) %collective-permute-start.31) | collective-permute-done | bytes 786464 | tf_op jit(solution)/shard_map/ppermute | solution.py:90
  268.0 14.7 %collective-permute-done.34 = bf16[2,128,1536]{2,1,0:T(8,128)(2,1)S(1)} collective-permute-done((bf16[2,128,1536]{2,1,0:T(8,128)(2,1)S(1)}, bf16[2,128,1536]{2,1,0:T(8,128)(2,1)S(1)}, u32[]{:S(2)}, u32[]{:S(2)}) %collective-permute-start.34) | collective-permute-done | bytes 786464 | tf_op jit(solution)/shard_map/ppermute | solution.py:90
  282.7 1.7 collective-permute-start.32
  286.1 25.0 %collective-permute-done.32 = bf16[1,128,1536]{2,1,0:T(8,128)(2,1)S(1)} collective-permute-done((bf16[1,128,1536]{2,1,0:T(8,128)(2,1)S(1)}, bf16[1,128,1536]{2,1,0:T(8,128)(2,1)S(1)}, u32[]{:S(2)}, u32[]{:S(2)}) %collective-permute-start.32) | collective-permute-done | bytes 393248 | tf_op jit(solution)/shard_map/ppermute | solution.py:90
  311.3 7.2 %collective-permute-done.35 = bf16[1,128,1536]{2,1,0:T(8,128)(2,1)S(1)} collective-permute-done((bf16[1,128,1536]{2,1,0:T(8,128)(2,1)S(1)}, bf16[1,128,1536]{2,1,0:T(8,128)(2,1)S(1)}, u32[]{:S(2)}, u32[]{:S(2)}) %collective-permute-start.35) | collective-permute-done | bytes 393248 | tf_op jit(solution)/shard_map/ppermute | solution.py:90
  320.6 2.5 reshape.519
  323.1 2.5 copy.142
  325.6 1.8 pad_maximum_fusion
  328.9 4.2 reshape.518
  333.1 4.1 fusion.89
  339.4 1.7 select_bitcast_fusion.3
  349.8 2.8 fusion
  352.6 2.9 fusion.2
  359.1 2.4 fusion.32
  361.6 3.8 multiply_reduce_fusion
  365.5 2.6 convolution_convert_fusion
  368.2 4.0 copy.132
  372.2 3.1 convolution_convert_fusion.1
  375.3 1.9 copy.134
  377.2 2.0 copy.135
  379.9 1.7 dynamic-slice_convert_fusion
  382.0 2.6 collective-permute-done.20
  386.9 2.2 collective-permute-done.21
  389.3 1.8 select_bitcast_fusion.5
  391.2 1.9 collective-permute-done.22
  396.8 2.0 collective-permute-done.23
  399.4 5.2 %collective-permute-done.16 = bf16[2,2,128,768]{2,3,0,1:T(8,128)(2,1)S(1)} collective-permute-done((bf16[2,2,128,768]{2,3,0,1:T(8,128)(2,1)S(1)}, bf16[2,2,128,768]{2,3,0,1:T(8,128)(2,1)S(1)}, u32[]{:S(2)}, u32[]{:S(2)}) %collective-permute-start.16) | collective-permute-done | bytes 786464 | tf_op jit(solution)/shard_map/ppermute | solution.py:90
  405.0 10.9 %collective-permute-done.14 = bf16[512,1024]{1,0:T(8,128)(2,1)S(1)} collective-permute-done((bf16[512,1024]{1,0:T(8,128)(2,1)S(1)}, bf16[512,1024]{1,0:T(8,128)(2,1)S(1)}, u32[]{:S(2)}, u32[]{:S(2)}) %collective-permute-start.14) | collective-permute-done | bytes 1048608 | tf_op jit(solution)/shard_map/ppermute | solution.py:75
  417.3 1.7 collective-permute-start.18
  419.6 10.2 %collective-permute-done.18 = bf16[128,768]{0,1:T(8,128)(2,1)S(1)} collective-permute-done((bf16[128,768]{0,1:T(8,128)(2,1)S(1)}, bf16[128,768]{0,1:T(8,128)(2,1)S(1)}, u32[]{:S(2)}, u32[]{:S(2)}) %collective-permute-start.18) | collective-permute-done | bytes 196640 | tf_op jit(solution)/shard_map/ppermute | solution.py:90
  (316 shorter events, 79.3 us)
Async XLA Ops:
  0.6 66.3 %copy-start = (bf16[1024,16]{0,1:T(8,128)(2,1)S(1)}, bf16[1024,16]{0,1:T(8,128)(2,1)}, u32[]{:S(2)}) copy-start(bf16[1024,16]{0,1:T(8,128)(2,1)} %param.23) | copy-start | bytes 98308
  0.7 6.4 %copy-start.25 = (bf16[1024,1024]{1,0:T(8,128)(2,1)S(1)}, bf16[1024,1024]{1,0:T(8,128)(2,1)}, u32[]{:S(2)}) copy-start(bf16[1024,1024]{1,0:T(8,128)(2,1)} %param.16) | copy-start | bytes 6291460
  0.7 6.4 %copy-start.63 = (f32[1024]{0:T(1024)S(1)}, f32[1024]{0:T(1024)}, u32[]{:S(2)}) copy-start(f32[1024]{0:T(1024)} %param.21) | copy-start | bytes 12292
  0.7 31.7 %collective-permute-start.2 = (bf16[256,1024]{1,0:T(8,128)(2,1)}, bf16[256,1024]{1,0:T(8,128)(2,1)}, u32[]{:S(2)}, u32[]{:S(2)}) collective-permute-start(bf16[256,1024]{1,0:T(8,128)(2,1)} %param.20), channel_id=1, source_target_pairs={{0,2},{1,3},{2,0},{3,1},{4,6},{5,7},{6,4},{7,5},{8,10},{9,11},{10,... | collective-permute-start | bytes 1572872 | tf_op jit(solution)/shard_map/ppermute | solution.py:335
  5.8 51.9 %copy-start.65 = (f32[1024]{0:T(1024)}, f32[1024]{0:T(1024)S(1)}, u32[]{:S(2)}) copy-start(f32[1024]{0:T(1024)S(1)} %add_rsqrt_fusion) | copy-start | bytes 12292
  11.7 5.2 %copy-start.41 = (bf16[1024,2,32]{0,2,1:T(8,128)(2,1)}, bf16[1024,2,32]{0,2,1:T(8,128)(2,1)S(1)}, u32[]{:S(2)}) copy-start(bf16[1024,2,32]{0,2,1:T(8,128)(2,1)S(1)} %get-tuple-element.121) | copy-start | bytes 393220
  13.9 13.9 %copy-start.23 = (pred[512,1024]{0,1:T(8,128)(4,1)}, pred[512,1024]{0,1:T(8,128)(4,1)S(1)}, u32[]{:S(2)}) copy-start(pred[512,1024]{0,1:T(8,128)(4,1)S(1)} %copy.113) | copy-start | bytes 1572868
  15.3 9.1 %copy-start.37 = (bf16[512,4,64]{0,2,1:T(8,128)(2,1)}, bf16[512,4,64]{0,2,1:T(8,128)(2,1)S(1)}, u32[]{:S(2)}) copy-start(bf16[512,4,64]{0,2,1:T(8,128)(2,1)S(1)} %get-tuple-element.127) | copy-start | bytes 786436
  24.4 5.0 %copy-start.16 = (f32[2,1024,512,2]{2,1,3,0:T(8,128)S(1)}, f32[2,1024,512,2]{2,1,3,0:T(8,128)}, u32[]{:S(2)}) copy-start(f32[2,1024,512,2]{2,1,3,0:T(8,128)} %copy-done.15) | copy-start | bytes 25165828
  25.3 9.2 %copy-start.17 = (f32[2,512,512,2]{2,1,3,0:T(8,128)}, f32[2,512,512,2]{2,1,3,0:T(8,128)S(1)}, u32[]{:S(2)}) copy-start(f32[2,512,512,2]{2,1,3,0:T(8,128)S(1)} %get-tuple-element.151) | copy-start | bytes 12582916
  27.8 6.7 %copy-start.52 = (bf16[512,128]{0,1:T(8,128)(2,1)}, bf16[512,128]{0,1:T(8,128)(2,1)S(1)}, u32[]{:S(2)}) copy-start(bf16[512,128]{0,1:T(8,128)(2,1)S(1)} %slice.273) | copy-start | bytes 393220
  34.5 5.5 %collective-permute-start.3 = (bf16[2,256,1024]{2,1,0:T(8,128)(2,1)}, bf16[2,256,1024]{2,1,0:T(8,128)(2,1)S(1)}, u32[]{:S(2)}, u32[]{:S(2)}) collective-permute-start(bf16[2,256,1024]{2,1,0:T(8,128)(2,1)} %pad_maximum_fusion.6), channel_id=1, source_target_pairs={{0,1},{1,0},{2,3},{3,2},{4,5},{5,4},{6,7},{7,6},{8,9},{9,8},{10,11... | collective-permute-start | bytes 3145736 | tf_op jit(solution)/shard_map/ppermute | solution.py:337
  37.5 1.7 collective-permute-start
  39.3 14.3 %collective-permute-start.1 = (bf16[512,512]{0,1:T(8,128)(2,1)S(1)}, bf16[512,512]{0,1:T(8,128)(2,1)S(1)}, u32[]{:S(2)}, u32[]{:S(2)}) collective-permute-start(bf16[512,512]{0,1:T(8,128)(2,1)S(1)} %pad_maximum_fusion.10), channel_id=1, source_target_pairs={{0,2},{1,3},{2,0},{3,1},{4,6},{5,7},{6,4},{7,5},{8,10},{9,11},{10,... | collective-permute-start | bytes 1572872 | tf_op jit(solution)/shard_map/ppermute | solution.py:383
  40.0 16.0 %copy-start.21 = (f32[1024,1024]{1,0:T(8,128)}, f32[1024,1024]{1,0:T(8,128)S(1)}, u32[]{:S(2)}) copy-start(f32[1024,1024]{1,0:T(8,128)S(1)} %convert_element_type.343) | copy-start | bytes 12582916
  40.0 13.6 %copy-start.56 = (bf16[256,1024]{1,0:T(8,128)(2,1)S(1)}, bf16[256,1024]{1,0:T(8,128)(2,1)}, u32[]{:S(2)}) copy-start(bf16[256,1024]{1,0:T(8,128)(2,1)} %param.20) | copy-start | bytes 1572868
  57.6 4.1 copy-start.32
  57.6 4.1 collective-permute-start.4
  57.8 105.9 %copy-start.61 = (f32[512]{0:T(512)}, f32[512]{0:T(512)S(1)}, u32[]{:S(2)}) copy-start(f32[512]{0:T(512)S(1)} %dynamic-slice.3) | copy-start | bytes 6148
  64.3 7.9 %copy-start.2 = (bf16[2,512,1024]{2,1,0:T(8,128)(2,1)}, bf16[2,512,1024]{2,1,0:T(8,128)(2,1)S(1)}, u32[]{:S(2)}) copy-start(bf16[2,512,1024]{2,1,0:T(8,128)(2,1)S(1)} %pad_maximum_fusion.1) | copy-start | bytes 6291460
  96.7 82.9 %collective-permute-start.24 = (bf16[4,128,1536]{2,1,0:T(8,128)(2,1)}, bf16[4,128,1536]{2,1,0:T(8,128)(2,1)}, u32[]{:S(2)}, u32[]{:S(2)}) collective-permute-start(bf16[4,128,1536]{2,1,0:T(8,128)(2,1)} %get-tuple-element.33), channel_id=1, source_target_pairs={{0,4},{4,0},{8,12},{12,8},{16,20},{20,16},{24,28},{28,24},{1,5},{5... | collective-permute-start | bytes 4718600 | tf_op jit(solution)/shard_map/ppermute | solution.py:90
  98.2 56.5 %copy-start.58 = (pred[1024,16]{1,0:T(8,128)(4,1)S(1)}, pred[1024,16]{1,0:T(8,128)(4,1)}, u32[]{:S(2)}) copy-start(pred[1024,16]{1,0:T(8,128)(4,1)} %get-tuple-element.156) | copy-start | bytes 49156
  154.7 7.3 %copy-start.7 = (bf16[4,128,1536]{2,1,0:T(8,128)(2,1)}, bf16[4,128,1536]{2,1,0:T(8,128)(2,1)S(1)}, u32[]{:S(2)}) copy-start(bf16[4,128,1536]{2,1,0:T(8,128)(2,1)S(1)} %get-tuple-element.34) | copy-start | bytes 4718596
  154.7 7.3 %copy-start.11 = (bf16[4,128,1536]{2,1,0:T(8,128)(2,1)}, bf16[4,128,1536]{2,1,0:T(8,128)(2,1)S(1)}, u32[]{:S(2)}) copy-start(bf16[4,128,1536]{2,1,0:T(8,128)(2,1)S(1)} %get-tuple-element.39) | copy-start | bytes 4718596
  154.7 7.3 %copy-start.13 = (bf16[4,128,1536]{2,1,0:T(8,128)(2,1)}, bf16[4,128,1536]{2,1,0:T(8,128)(2,1)S(1)}, u32[]{:S(2)}) copy-start(bf16[4,128,1536]{2,1,0:T(8,128)(2,1)S(1)} %get-tuple-element.37) | copy-start | bytes 4718596
  154.8 7.6 %collective-permute-start.10 = (bf16[512,16]{1,0:T(8,128)(2,1)S(1)}, bf16[512,16]{1,0:T(8,128)(2,1)S(1)}, u32[]{:S(2)}, u32[]{:S(2)}) collective-permute-start(bf16[512,16]{1,0:T(8,128)(2,1)S(1)} %dynamic-slice_convert_fusion.3), channel_id=1, source_target_pairs={{0,1},{1,0},{2,3},{3,2},{4,5},{5,4},{6,7},{7,6},{8,9},{9,8},{10,11... | collective-permute-start | bytes 49160 | tf_op jit(solution)/shard_map/ppermute | solution.py:73
  159.1 14.4 %collective-permute-start.8 = (bf16[512,1024]{1,0:T(8,128)(2,1)}, bf16[512,1024]{1,0:T(8,128)(2,1)}, u32[]{:S(2)}, u32[]{:S(2)}) collective-permute-start(bf16[512,1024]{1,0:T(8,128)(2,1)} %dynamic-slice_convert_fusion.1), channel_id=1, source_target_pairs={{0,1},{1,0},{2,3},{3,2},{4,5},{5,4},{6,7},{7,6},{8,9},{9,8},{10,11... | collective-permute-start | bytes 3145736 | tf_op jit(solution)/shard_map/ppermute | solution.py:73
  162.1 15.3 %collective-permute-start.5 = (bf16[512,1024]{1,0:T(8,128)(2,1)}, bf16[512,1024]{1,0:T(8,128)(2,1)}, u32[]{:S(2)}, u32[]{:S(2)}) collective-permute-start(bf16[512,1024]{1,0:T(8,128)(2,1)} %dynamic-slice_convert_fusion.2), channel_id=1, source_target_pairs={{0,1},{1,0},{2,3},{3,2},{4,5},{5,4},{6,7},{7,6},{8,9},{9,8},{10,11... | collective-permute-start | bytes 3145736 | tf_op jit(solution)/shard_map/ppermute | solution.py:73
  163.1 5.9 %collective-permute-start.11 = (bf16[512,16]{1,0:T(8,128)(2,1)}, bf16[512,16]{1,0:T(8,128)(2,1)}, u32[]{:S(2)}, u32[]{:S(2)}) collective-permute-start(bf16[512,16]{1,0:T(8,128)(2,1)} %add_convert_fusion.23), channel_id=1, source_target_pairs={{0,2},{1,3},{2,0},{3,1},{4,6},{5,7},{6,4},{7,5},{8,10},{9,11},{10,... | collective-permute-start | bytes 49160 | tf_op jit(solution)/shard_map/ppermute | solution.py:75
  164.3 9.2 %copy-start.12 = (bf16[4,128,1536]{2,1,0:T(8,128)(2,1)S(1)}, bf16[4,128,1536]{2,1,0:T(8,128)(2,1)}, u32[]{:S(2)}) copy-start(bf16[4,128,1536]{2,1,0:T(8,128)(2,1)} %copy-done.11) | copy-start | bytes 4718596
  164.3 36.4 %collective-permute-start.27 = (bf16[4,128,1536]{2,1,0:T(8,128)(2,1)}, bf16[4,128,1536]{2,1,0:T(8,128)(2,1)S(1)}, u32[]{:S(2)}, u32[]{:S(2)}) collective-permute-start(bf16[4,128,1536]{2,1,0:T(8,128)(2,1)} %copy-done.14), channel_id=1, source_target_pairs={{0,8},{4,12},{8,0},{12,4},{16,24},{20,28},{24,16},{28,20},{1,9},{5... | collective-permute-start | bytes 4718600 | tf_op jit(solution)/shard_map/ppermute | solution.py:90
  169.0 37.5 %collective-permute-start.30 = (bf16[4,128,1536]{2,1,0:T(8,128)(2,1)}, bf16[4,128,1536]{2,1,0:T(8,128)(2,1)S(1)}, u32[]{:S(2)}, u32[]{:S(2)}) collective-permute-start(bf16[4,128,1536]{2,1,0:T(8,128)(2,1)} %copy-done.13), channel_id=1, source_target_pairs={{0,4},{4,0},{8,12},{12,8},{16,20},{20,16},{24,28},{28,24},{1,5},{5... | collective-permute-start | bytes 4718600 | tf_op jit(solution)/shard_map/ppermute | solution.py:90
  173.5 4.5 %copy-start.35 = (f32[1024,1024]{1,0:T(8,128)S(1)}, f32[1024,1024]{1,0:T(8,128)}, u32[]{:S(2)}) copy-start(f32[1024,1024]{1,0:T(8,128)} %get-tuple-element.28) | copy-start | bytes 12582916
  173.5 65.1 %collective-permute-start.33 = (bf16[4,128,1536]{2,1,0:T(8,128)(2,1)S(1)}, bf16[4,128,1536]{2,1,0:T(8,128)(2,1)S(1)}, u32[]{:S(2)}, u32[]{:S(2)}) collective-permute-start(bf16[4,128,1536]{2,1,0:T(8,128)(2,1)S(1)} %copy-done.12), channel_id=1, source_target_pairs={{0,4},{4,0},{8,12},{12,8},{16,20},{20,16},{24,28},{28,24},{1,5},{5... | collective-permute-start | bytes 4718600 | tf_op jit(solution)/shard_map/ppermute | solution.py:90
  177.4 63.2 %collective-permute-start.9 = (bf16[512,1024]{1,0:T(8,128)(2,1)S(1)}, bf16[512,1024]{1,0:T(8,128)(2,1)S(1)}, u32[]{:S(2)}, u32[]{:S(2)}) collective-permute-start(bf16[512,1024]{1,0:T(8,128)(2,1)S(1)} %add_convert_fusion.1), channel_id=1, source_target_pairs={{0,2},{1,3},{2,0},{3,1},{4,6},{5,7},{6,4},{7,5},{8,10},{9,11},{10,... | collective-permute-start | bytes 3145736 | tf_op jit(solution)/shard_map/ppermute | solution.py:75
  179.6 63.0 %collective-permute-start.6 = (bf16[512,1024]{1,0:T(8,128)(2,1)S(1)}, bf16[512,1024]{1,0:T(8,128)(2,1)S(1)}, u32[]{:S(2)}, u32[]{:S(2)}) collective-permute-start(bf16[512,1024]{1,0:T(8,128)(2,1)S(1)} %add_convert_fusion.3), channel_id=1, source_target_pairs={{0,2},{1,3},{2,0},{3,1},{4,6},{5,7},{6,4},{7,5},{8,10},{9,11},{10,... | collective-permute-start | bytes 3145736 | tf_op jit(solution)/shard_map/ppermute | solution.py:75
  181.2 21.1 %copy-start.8 = (bf16[4,128,1536]{2,1,0:T(8,128)(2,1)S(1)}, bf16[4,128,1536]{2,1,0:T(8,128)(2,1)}, u32[]{:S(2)}) copy-start(bf16[4,128,1536]{2,1,0:T(8,128)(2,1)} %copy-done.7) | copy-start | bytes 4718596
  200.7 44.5 %collective-permute-start.25 = (bf16[2,128,1536]{2,1,0:T(8,128)(2,1)S(1)}, bf16[2,128,1536]{2,1,0:T(8,128)(2,1)S(1)}, u32[]{:S(2)}, u32[]{:S(2)}) collective-permute-start(bf16[2,128,1536]{2,1,0:T(8,128)(2,1)S(1)} %get-tuple-element.95), channel_id=1, source_target_pairs={{0,8},{4,12},{8,0},{12,4},{16,24},{20,28},{24,16},{28,20},{1,9},{5... | collective-permute-start | bytes 2359304 | tf_op jit(solution)/shard_map/ppermute | solution.py:90
  206.5 39.3 %collective-permute-start.28 = (bf16[2,128,1536]{2,1,0:T(8,128)(2,1)S(1)}, bf16[2,128,1536]{2,1,0:T(8,128)(2,1)S(1)}, u32[]{:S(2)}, u32[]{:S(2)}) collective-permute-start(bf16[2,128,1536]{2,1,0:T(8,128)(2,1)S(1)} %get-tuple-element.97), channel_id=1, source_target_pairs={{0,16},{4,20},{8,24},{12,28},{16,0},{20,4},{24,8},{28,12},{1,17},{... | collective-permute-start | bytes 2359304 | tf_op jit(solution)/shard_map/ppermute | solution.py:90
  238.6 28.8 %collective-permute-start.31 = (bf16[2,128,1536]{2,1,0:T(8,128)(2,1)S(1)}, bf16[2,128,1536]{2,1,0:T(8,128)(2,1)S(1)}, u32[]{:S(2)}, u32[]{:S(2)}) collective-permute-start(bf16[2,128,1536]{2,1,0:T(8,128)(2,1)S(1)} %get-tuple-element.99), channel_id=1, source_target_pairs={{0,8},{4,12},{8,0},{12,4},{16,24},{20,28},{24,16},{28,20},{1,9},{5... | collective-permute-start | bytes 2359304 | tf_op jit(solution)/shard_map/ppermute | solution.py:90
  240.6 42.2 %collective-permute-start.34 = (bf16[2,128,1536]{2,1,0:T(8,128)(2,1)S(1)}, bf16[2,128,1536]{2,1,0:T(8,128)(2,1)S(1)}, u32[]{:S(2)}, u32[]{:S(2)}) collective-permute-start(bf16[2,128,1536]{2,1,0:T(8,128)(2,1)S(1)} %get-tuple-element.101), channel_id=1, source_target_pairs={{0,8},{4,12},{8,0},{12,4},{16,24},{20,28},{24,16},{28,20},{1,9},{5... | collective-permute-start | bytes 2359304 | tf_op jit(solution)/shard_map/ppermute | solution.py:90
  245.1 94.3 %collective-permute-start.12 = (bf16[512,1024]{1,0:T(8,128)(2,1)}, bf16[512,1024]{1,0:T(8,128)(2,1)}, u32[]{:S(2)}, u32[]{:S(2)}) collective-permute-start(bf16[512,1024]{1,0:T(8,128)(2,1)} %get-tuple-element.90), channel_id=1, source_target_pairs={{0,1},{1,0},{2,3},{3,2},{4,5},{5,4},{6,7},{7,6},{8,9},{9,8},{10,11... | collective-permute-start | bytes 3145736 | tf_op jit(solution)/shard_map/ppermute | solution.py:80
  245.2 144.2 %collective-permute-start.7 = (bf16[512,1024]{1,0:T(8,128)(2,1)}, bf16[512,1024]{1,0:T(8,128)(2,1)}, u32[]{:S(2)}, u32[]{:S(2)}) collective-permute-start(bf16[512,1024]{1,0:T(8,128)(2,1)} %get-tuple-element.108), channel_id=1, source_target_pairs={{0,1},{1,0},{2,3},{3,2},{4,5},{5,4},{6,7},{7,6},{8,9},{9,8},{10,11... | collective-permute-start | bytes 3145736 | tf_op jit(solution)/shard_map/ppermute | solution.py:80
  245.8 38.7 %collective-permute-start.26 = (bf16[1,128,1536]{2,1,0:T(8,128)(2,1)S(1)}, bf16[1,128,1536]{2,1,0:T(8,128)(2,1)S(1)}, u32[]{:S(2)}, u32[]{:S(2)}) collective-permute-start(bf16[1,128,1536]{2,1,0:T(8,128)(2,1)S(1)} %add_convert_fusion.18), channel_id=1, source_target_pairs={{0,16},{4,20},{8,24},{12,28},{16,0},{20,4},{24,8},{28,12},{1,17},{... | collective-permute-start | bytes 1179656 | tf_op jit(solution)/shard_map/ppermute | solution.py:90
  267.4 18.5 %collective-permute-start.29 = (bf16[1,128,1536]{2,1,0:T(8,128)(2,1)S(1)}, bf16[1,128,1536]{2,1,0:T(8,128)(2,1)S(1)}, u32[]{:S(2)}, u32[]{:S(2)}) collective-permute-start(bf16[1,128,1536]{2,1,0:T(8,128)(2,1)S(1)} %add_convert_fusion.16), channel_id=1, source_target_pairs={{0,4},{4,0},{8,12},{12,8},{16,20},{20,16},{24,28},{28,24},{1,5},{5... | collective-permute-start | bytes 1179656 | tf_op jit(solution)/shard_map/ppermute | solution.py:90
  282.7 28.4 %collective-permute-start.32 = (bf16[1,128,1536]{2,1,0:T(8,128)(2,1)S(1)}, bf16[1,128,1536]{2,1,0:T(8,128)(2,1)S(1)}, u32[]{:S(2)}, u32[]{:S(2)}) collective-permute-start(bf16[1,128,1536]{2,1,0:T(8,128)(2,1)S(1)} %add_convert_fusion.14), channel_id=1, source_target_pairs={{0,16},{4,20},{8,24},{12,28},{16,0},{20,4},{24,8},{28,12},{1,17},{... | collective-permute-start | bytes 1179656 | tf_op jit(solution)/shard_map/ppermute | solution.py:90
  284.5 34.0 %collective-permute-start.35 = (bf16[1,128,1536]{2,1,0:T(8,128)(2,1)S(1)}, bf16[1,128,1536]{2,1,0:T(8,128)(2,1)S(1)}, u32[]{:S(2)}, u32[]{:S(2)}) collective-permute-start(bf16[1,128,1536]{2,1,0:T(8,128)(2,1)S(1)} %add_convert_fusion.12), channel_id=1, source_target_pairs={{0,16},{4,20},{8,24},{12,28},{16,0},{20,4},{24,8},{28,12},{1,17},{... | collective-permute-start | bytes 1179656 | tf_op jit(solution)/shard_map/ppermute | solution.py:90
  286.1 32.5 %copy-start.28 = (f32[1,128,1536]{2,1,0:T(8,128)}, f32[1,128,1536]{2,1,0:T(8,128)S(1)}, u32[]{:S(2)}) copy-start(f32[1,128,1536]{2,1,0:T(8,128)S(1)} %convert_add_fusion.4) | copy-start | bytes 2359300
  311.3 7.4 %copy-start.29 = (f32[1,128,1536]{2,1,0:T(8,128)}, f32[1,128,1536]{2,1,0:T(8,128)S(1)}, u32[]{:S(2)}) copy-start(f32[1,128,1536]{2,1,0:T(8,128)S(1)} %convert_add_fusion.3) | copy-start | bytes 2359300
  368.1 11.2 %collective-permute-start.19 = (f32[18,1024]{1,0:T(8,128)S(1)}, f32[18,1024]{1,0:T(8,128)S(1)}, u32[]{:S(2)}, u32[]{:S(2)}) collective-permute-start(f32[18,1024]{1,0:T(8,128)S(1)} %pad_maximum_fusion.17), channel_id=1, source_target_pairs={{0,1},{1,0},{2,3},{3,2},{4,5},{5,4},{6,7},{7,6},{8,9},{9,8},{10,11... | collective-permute-start | bytes 221192 | tf_op jit(solution)/shard_map/ppermute | solution.py:485
  379.3 6.0 %copy-start.31 = (bf16[2,2,2,128,256]{3,4,0,1,2:T(8,128)(2,1)S(1)}, bf16[2,2,2,128,256]{3,4,0,1,2:T(8,128)(2,1)}, u32[]{:S(2)}) copy-start(bf16[2,2,2,128,256]{3,4,0,1,2:T(8,128)(2,1)} %copy.135) | copy-start | bytes 1572868
  379.3 5.2 %collective-permute-start.20 = (f32[18,1024]{1,0:T(8,128)S(1)}, f32[18,1024]{1,0:T(8,128)S(1)}, u32[]{:S(2)}, u32[]{:S(2)}) collective-permute-start(f32[18,1024]{1,0:T(8,128)S(1)} %fusion.124), channel_id=1, source_target_pairs={{0,2},{1,3},{2,0},{3,1},{4,6},{5,7},{6,4},{7,5},{8,10},{9,11},{10,... | collective-permute-start | bytes 221192 | tf_op jit(solution)/shard_map/ppermute | solution.py:486
  381.7 11.4 %collective-permute-start.13 = (bf16[512,1024]{1,0:T(8,128)(2,1)S(1)}, bf16[512,1024]{1,0:T(8,128)(2,1)S(1)}, u32[]{:S(2)}, u32[]{:S(2)}) collective-permute-start(bf16[512,1024]{1,0:T(8,128)(2,1)S(1)} %dynamic-slice_convert_fusion), channel_id=1, source_target_pairs={{0,1},{1,0},{2,3},{3,2},{4,5},{5,4},{6,7},{7,6},{8,9},{9,8},{10,11... | collective-permute-start | bytes 3145736 | tf_op jit(solution)/shard_map/ppermute | solution.py:73
  384.7 4.4 %collective-permute-start.21 = (f32[2,2,18,128]{3,1,2,0:T(2,128)S(1)}, f32[2,2,18,128]{3,1,2,0:T(2,128)S(1)}, u32[]{:S(2)}, u32[]{:S(2)}) collective-permute-start(f32[2,2,18,128]{3,1,2,0:T(2,128)S(1)} %bitcast.303), channel_id=1, source_target_pairs={{0,4},{4,0},{8,12},{12,8},{16,20},{20,16},{24,28},{28,24},{1,5},{5... | collective-permute-start | bytes 110600 | tf_op jit(solution)/shard_map/ppermute | solution.py:90
  385.4 19.3 %collective-permute-start.16 = (bf16[2,2,128,768]{2,3,0,1:T(8,128)(2,1)S(1)}, bf16[2,2,128,768]{2,3,0,1:T(8,128)(2,1)S(1)}, u32[]{:S(2)}, u32[]{:S(2)}) collective-permute-start(bf16[2,2,128,768]{2,3,0,1:T(8,128)(2,1)S(1)} %fusion.56), channel_id=1, source_target_pairs={{0,4},{4,0},{8,12},{12,8},{16,20},{20,16},{24,28},{28,24},{1,5},{5... | collective-permute-start | bytes 2359304 | tf_op jit(solution)/shard_map/ppermute | solution.py:90
  389.2 3.8 collective-permute-start.22
  393.5 22.4 %collective-permute-start.14 = (bf16[512,1024]{1,0:T(8,128)(2,1)S(1)}, bf16[512,1024]{1,0:T(8,128)(2,1)S(1)}, u32[]{:S(2)}, u32[]{:S(2)}) collective-permute-start(bf16[512,1024]{1,0:T(8,128)(2,1)S(1)} %add_convert_fusion), channel_id=1, source_target_pairs={{0,2},{1,3},{2,0},{3,1},{4,6},{5,7},{6,4},{7,5},{8,10},{9,11},{10,... | collective-permute-start | bytes 3145736 | tf_op jit(solution)/shard_map/ppermute | solution.py:75
  394.2 4.7 %collective-permute-start.23 = (f32[18,128]{1,0:T(8,128)S(1)}, f32[18,128]{1,0:T(8,128)S(1)}, u32[]{:S(2)}, u32[]{:S(2)}) collective-permute-start(f32[18,128]{1,0:T(8,128)S(1)} %bitcast.309), channel_id=1, source_target_pairs={{0,16},{4,20},{8,24},{12,28},{16,0},{20,4},{24,8},{28,12},{1,17},{... | collective-permute-start | bytes 27656 | tf_op jit(solution)/shard_map/ppermute | solution.py:90
  395.3 20.5 %copy-start.22 = (f32[1024,1024]{1,0:T(8,128)S(1)}, f32[1024,1024]{1,0:T(8,128)}, u32[]{:S(2)}) copy-start(f32[1024,1024]{1,0:T(8,128)} %copy-done.21) | copy-start | bytes 12582916
  404.9 11.5 %copy-start.62 = (f32[512]{0:T(512)S(1)}, f32[512]{0:T(512)}, u32[]{:S(2)}) copy-start(f32[512]{0:T(512)} %copy-done.61) | copy-start | bytes 6148
  404.9 11.5 %copy-start.67 = (f32[512,1]{0,1:T(1,128)S(1)}, f32[512,1]{0,1:T(1,128)}, u32[]{:S(2)}) copy-start(f32[512,1]{0,1:T(1,128)} %multiply_multiply_fusion) | copy-start | bytes 6148
  404.9 12.2 %collective-permute-start.17 = (bf16[2,128,768]{1,2,0:T(8,128)(2,1)S(1)}, bf16[2,128,768]{1,2,0:T(8,128)(2,1)S(1)}, u32[]{:S(2)}, u32[]{:S(2)}) collective-permute-start(bf16[2,128,768]{1,2,0:T(8,128)(2,1)S(1)} %dynamic-slice_bitcast_fusion), channel_id=1, source_target_pairs={{0,8},{4,12},{8,0},{12,4},{16,24},{20,28},{24,16},{28,20},{1,9},{5... | collective-permute-start | bytes 1179656 | tf_op jit(solution)/shard_map/ppermute | solution.py:90
  417.1 15.6 %collective-permute-start.15 = (bf16[512,1024]{1,0:T(8,128)(2,1)S(1)}, bf16[512,1024]{1,0:T(8,128)(2,1)S(1)}, u32[]{:S(2)}, u32[]{:S(2)}) collective-permute-start(bf16[512,1024]{1,0:T(8,128)(2,1)S(1)} %subtract_convert_fusion), channel_id=1, source_target_pairs={{0,1},{1,0},{2,3},{3,2},{4,5},{5,4},{6,7},{7,6},{8,9},{9,8},{10,11... | collective-permute-start | bytes 3145736 | tf_op jit(solution)/shard_map/ppermute | solution.py:80
  417.3 12.4 %collective-permute-start.18 = (bf16[128,768]{0,1:T(8,128)(2,1)S(1)}, bf16[128,768]{0,1:T(8,128)(2,1)S(1)}, u32[]{:S(2)}, u32[]{:S(2)}) collective-permute-start(bf16[128,768]{0,1:T(8,128)(2,1)S(1)} %dynamic-slice_bitcast_fusion.1), channel_id=1, source_target_pairs={{0,16},{4,20},{8,24},{12,28},{16,0},{20,4},{24,8},{28,12},{1,17},{... | collective-permute-start | bytes 589832 | tf_op jit(solution)/shard_map/ppermute | solution.py:90
  (50 other events, 113.1 us)
